TPU v7x, 32 devices: a whole 2x2x4 slice. The times are simulated.
32 devices in a mesh: frame: 8 (over y, x, core), row: 4 (over z).
Axes of the slice: x: 2, y: 2, z: 4, core: 2. Of those that a mesh axis runs over, the one named last changes fastest.
Arguments:
- tokens: bfloat16 [8, 512, 2048], P('frame', 'row'), may hold values from -6 to 6
- w_gate: bfloat16 [2048, 4096], P(None, 'row'), may hold values from -0.125 to 0.125
- w_value: bfloat16 [2048, 4096], P(None, 'row'), may hold values from -0.125 to 0.125
- w_state_proj: bfloat16 [2048, 512], replicated, may hold values from -0.03125 to 0.03125
- w_step: bfloat16 [2, 2048, 64], P(None, None, 'row'), may hold values from -0.125 to 0.125
- step_bias: float32 [2, 64], P(None, 'row'), may hold values from -3 to 0
- decay_rate: float32 [2, 64], P(None, 'row'), may hold values from 0 to 0.3, as said below
- conv_taps: float32 [2, 4, 4096], P(None, None, 'row'), may hold values from -3 to 3
- skip_gain: float32 [2, 64], P(None, 'row'), may hold values from 0.1 to 16, as said below
- norm_gain: float32 [4096], P('row'), may hold values from 0.1 to 1.9
- w_out: bfloat16 [4096, 2048], P('row'), may hold values from -0.09375 to 0.09375
Outputs:
- mixed: bfloat16 [8, 512, 2048], P('frame', 'row')
Inputs may be any that keep to these rules, and one draw needn't show every extreme that they name: `decay_rate`: positive decay rates. `skip_gain`: positive skip weights.
All inputs are finite; a program needn't handle non-finite values.
Results may differ from a plain program's by a relative error of at most 0.015.
Values may be sent and summed in bfloat16 or wider, within the bound.
No kernel may reach another device: no remote copies, remote signals or barrier semaphores. Data moves between devices by JAX's collectives and lax.ppermute only.
A program may use at most 128 MiB of HBM per device.

v0:
```python
import math

import jax
import jax.numpy as jnp
from jax import lax
from jax.experimental import pallas as pl
from jax.experimental.pallas import tpu as pltpu
from jax.sharding import PartitionSpec as P


HEAD_DIM = 64
LANES = 128
LOGS = 8
SPLIT = 20_000_000_000
LOG2E = 1.0 / math.log(2.0)
F32 = jnp.float32
BF16 = jnp.bfloat16


def mib(size):
    return pltpu.CompilerParams(vmem_limit_bytes=size << 20)


def vmem():
    return pl.BlockSpec(memory_space=pltpu.VMEM)


def smem():
    return pl.BlockSpec(memory_space=pltpu.SMEM)


def dot(a, b):
    return jnp.dot(a, b, preferred_element_type=F32)


def silu(v):
    return v / (1.0 + jnp.exp(-v))


def two_parts(v, stride):
    high = v.astype(BF16).astype(F32)
    return (high + pltpu.roll(v - high, stride, 1)).astype(BF16)


def split(where, own, ring, edge):
    rows, depth = own.shape
    half = rows // 2

    def body(where, own, a, b, outer):
        a[...] = own[:half, :]
        b[...] = own[half:, :]

        @pl.when(where[0] == ring - 1)
        def _():
            outer[...] = own[rows - edge :, :]

        @pl.when(where[0] != ring - 1)
        def _():
            outer[...] = own[:edge, :]

    shapes = [(half, depth), (half, depth), (edge, depth)]
    return pl.pallas_call(
        body,
        in_specs=[smem(), vmem()],
        out_specs=[vmem()] * 3,
        out_shape=[jax.ShapeDtypeStruct(s, BF16) for s in shapes],
        compiler_params=mib(8),
        cost_estimate=pl.CostEstimate(flops=SPLIT, bytes_accessed=2 << 20, transcendentals=0),
        name="split",
    )(where, own)


def prepare(step_bias, decay_rate, skip_gain, channels):
    heads = step_bias.shape[1]
    rest = LANES - 2 * heads

    def body(bias, rate, skip, spread, rows, skips):
        lane = lax.broadcasted_iota(jnp.int32, (LANES, channels), 0)
        head = lax.shift_right_logical(
            lax.broadcasted_iota(jnp.int32, (LANES, channels), 1), HEAD_DIM.bit_length() - 1
        )
        for d in range(2):
            hit = (lane == head + d * heads) | (lane == head + (2 + d) * heads)
            spread[d] = jnp.where(hit, 1.0, 0.0).astype(BF16)
        zeros = jnp.zeros((1, rest), F32)
        for at, ref in enumerate((bias, rate)):
            rows[at : at + 1, :] = jnp.concatenate([ref[0:1, :], ref[1:2, :], zeros], axis=1)
        pieces = jnp.concatenate([skip[...], jnp.zeros((2, LANES - heads), F32)], axis=1)
        p1 = pieces.astype(BF16).astype(F32)
        p2 = (pieces - p1).astype(BF16).astype(F32)
        p3 = pieces - p1 - p2
        stack = jnp.concatenate([p1, p2, p3, jnp.zeros((10, LANES), F32)], axis=0).astype(BF16)
        wide = dot(stack, spread[0])
        skips[...] = wide[0:2] + wide[2:4] + wide[4:6]

    shapes = [((2, LANES, channels), BF16), ((2, LANES), F32), ((2, channels), F32)]
    return pl.pallas_call(
        body,
        in_specs=[vmem()] * 3,
        out_specs=[vmem()] * 3,
        out_shape=[jax.ShapeDtypeStruct(*s) for s in shapes],
        compiler_params=mib(8),
        name="prepare",
    )(step_bias, decay_rate, skip_gain)


def gather(refs, stacked):
    at = 0
    for ref in refs:
        stacked[at : at + ref.shape[0], :] = ref[...]
        at += ref.shape[0]


def conv_of(window, taps, backward, count):
    reach = taps.shape[0] - 1
    total = 0.0
    for j in range(reach + 1):
        start = reach - j if backward else j
        total = total + taps[j : j + 1] * window[start : start + count]
    return silu(total)


def block_states(pieces, bounds, where, w_value, w_state, w_step, taps, small_rows, heads):
    rows, depth = sum(p.shape[0] for p in pieces), pieces[0].shape[1]
    channels, states, steps = w_value.shape[1], w_state.shape[1], w_step.shape[0]
    size = states // 4
    reach = taps.shape[1] - 1
    count, around = len(pieces), len(bounds)
    pad = 8
    total = rows + (2 * pad if around else 0)

    def body(where, *refs):
        src, refs = refs[:count], refs[count:]
        edges, refs = refs[:around], refs[around:]
        wv, ws, wt, taps, small = refs[:5]
        xf, xb, ends, bc, b_t, cum_out, cum_t, reached, fade, last_out = refs[5:15]
        stacked, sx = refs[-2:]
        gather(src, stacked)
        for j, ref in enumerate(edges):

            @pl.when(lax.rem(where[0] + 1, around) == j)
            def _(ref=ref):
                stacked[rows : rows + pad, :] = ref[...]

            @pl.when(where[0] == j)
            def _(ref=ref):
                stacked[rows + pad :, :] = ref[...]

        sx[:pad, :] = jnp.zeros((pad, channels), F32)
        sx[pad + rows :, :] = jnp.zeros((pad, channels), F32)

        def conv(n):
            for at in range(n, n + 256, LANES):
                cols = slice(at, at + LANES)
                ahead, behind = taps[0, :, cols], taps[1, :, cols]
                for base in range(pad, pad + rows, 64):
                    views = {o: sx[base + o : base + o + 64, cols] for o in range(-reach, reach + 1)}
                    f = sum(ahead[j : j + 1] * views[j - reach] for j in range(reach + 1))
                    b = sum(behind[j : j + 1] * views[reach - j] for j in range(reach + 1))
                    xf[base - pad : base - pad + 64, cols] = silu(f).astype(BF16)
                    xb[base - pad : base - pad + 64, cols] = silu(b).astype(BF16)

        for n in range(0, channels, 256):
            cols = slice(n, n + 256)
            x = dot(stacked[...], wv[:, cols]).astype(BF16)
            sx[pad : pad + rows, cols] = x[:rows].astype(F32)
            ends[:pad, cols] = x[:pad]
            ends[pad : 2 * pad, cols] = x[rows - pad : rows]
            if around:
                ends[2 * pad :, cols] = x[rows:]
            if n:
                conv(n - 256)
        raw = lax.dot_general(
            stacked[:rows, :], wt[...], (((1,), (1,)), ((), ())), preferred_element_type=F32
        )
        raw = jnp.concatenate(
            [raw.astype(BF16).astype(F32), jnp.zeros((rows, LANES - steps), F32)], axis=1
        )
        for n in range(0, states, 256):
            bc[:, n : n + 256] = dot(stacked[:rows, :], ws[:, n : n + 256]).astype(BF16)
        conv(channels - 256)

        lane = lax.broadcasted_iota(jnp.int32, (rows, LANES), 1)
        used, forward = lane < 2 * heads, lane < heads
        low_row, low_col = (lax.broadcasted_iota(jnp.int32, (rows, rows), d) for d in (0, 1))
        both = jnp.concatenate(
            [
                jnp.where(low_row >= low_col, 1.0, 0.0).astype(BF16),
                jnp.where(low_row <= low_col, 1.0, 0.0).astype(BF16),
            ],
            axis=0,
        )
        v = raw + small[0:1, :]
        dt = jnp.maximum(v, 0.0) + jnp.log1p(jnp.exp(-jnp.abs(v)))
        dt = jnp.where(used, dt, 0.0)
        a = -dt * small[1:2, :] * LOG2E
        a1 = a.astype(BF16).astype(F32)
        a2 = (a - a1).astype(BF16).astype(F32)
        a3 = a - a1 - a2
        parts = a1 + pltpu.roll(a2, 2 * heads, 1) + pltpu.roll(a3, 4 * heads, 1)
        sums = dot(both, parts.astype(BF16))
        sums = pltpu.roll(sums, LANES - 4 * heads, 1) + pltpu.roll(sums, LANES - 2 * heads, 1) + sums
        cum = jnp.where(used, jnp.where(forward, sums[:rows], sums[rows:]), 0.0)
        last = jnp.where(forward[:1], cum[rows - 1 :], cum[:1])
        last_out[...] = jnp.broadcast_to(last, last_out.shape)
        cum_out[...] = cum
        cum_t[...] = (cum + pltpu.roll(dt, 2 * heads, 1)).T
        reached[...] = two_parts(jnp.where(used, jnp.exp2(cum), 0.0), 2 * heads)
        fade[...] = jnp.exp2(last - cum) * dt
        for d in range(2):
            b_t[d] = bc[:, d * 2 * size : (2 * d + 1) * size].astype(F32).T.astype(BF16)

    shapes = [
        ((rows, channels), BF16),
        ((rows, channels), BF16),
        ((4 * pad if around else 2 * pad, channels), BF16),
        ((rows, states), BF16),
        ((2, size, rows), BF16),
        ((rows, LANES), F32),
        ((LANES, rows), F32),
        ((rows, LANES), BF16),
        ((rows, LANES), F32),
        ((8, LANES), F32),
    ]
    width = channels + states + LANES
    return pl.pallas_call(
        body,
        in_specs=[smem()] + [vmem()] * (count + around + 5),
        out_specs=[vmem()] * len(shapes),
        out_shape=[jax.ShapeDtypeStruct(*s) for s in shapes],
        scratch_shapes=[
            pltpu.VMEM((total, depth), BF16),
            pltpu.VMEM((rows + 2 * pad, channels), F32),
        ],
        compiler_params=mib(16),
        cost_estimate=pl.CostEstimate(
            flops=3 * total * depth * width, bytes_accessed=2 * depth * width, transcendentals=0
        ),
        name="block_states",
    )(where, *pieces, *bounds, w_value, w_state, w_step, taps, small_rows)


def frame_logs(where, lasts, ring):
    at = [lax.rem(where[0] + k, ring) for k in range(ring)]
    rows = [ref[0:1, :] for ref in lasts]

    def between(low, high):
        out = jnp.zeros_like(rows[0])
        for place, row in zip(at, rows):
            out += jnp.where(jnp.logical_and(place > low, place < high), row, 0.0)
        return out

    return at, rows, between


def spread_rows(rows, heads, spread):
    lane = lax.broadcasted_iota(jnp.int32, rows[0].shape, 1)
    rows = [jnp.where(lane < 2 * heads, jnp.exp2(r), 0.0) for r in rows]
    short = -len(rows) % 8
    if short:
        rows.append(jnp.zeros((short, LANES), F32))
    packed = two_parts(jnp.concatenate(rows, axis=0), 2 * heads)
    return [dot(packed, spread[d]) for d in range(2)]


def combine(where, xfs, xbs, ends, b_ts, fades, lasts, taps, spread, heads):
    ring = len(xfs)
    rows, channels = xfs[0].shape
    size = b_ts[0].shape[1]
    pad = 8
    reach = taps.shape[1] - 1

    def body(where, *refs):
        xf, xb, ends, b_t, fades, lasts = (refs[i * ring : (i + 1) * ring] for i in range(6))
        taps, spread, pack, fixed, qs, carried, b_all = refs[6 * ring :]
        at, logs, between = frame_logs(where, lasts, ring)
        forward = lax.broadcasted_iota(jnp.int32, logs[0].shape, 1) < heads
        for k in range(ring):
            later = jnp.where(forward, between(at[k], ring), between(-1, at[k]))
            qs[k * rows : (k + 1) * rows, :] = two_parts(fades[k][...] * jnp.exp2(later), 2 * heads)
            for d in range(2):
                b_all[d, :, k * rows : (k + 1) * rows] = b_t[k][d]
            first, final = at[k] == 0, at[k] == ring - 1
            below, above = ends[(k - 1) % ring], ends[(k + 1) % ring]
            for n in range(0, channels, 256):
                cols = slice(n, n + 256)
                own = ends[k][: 2 * pad, cols].astype(F32)
                before = jnp.where(first, ends[1][2 * pad : 3 * pad, cols], below[pad : 2 * pad, cols])
                after = jnp.where(final, ends[1][3 * pad :, cols], above[:pad, cols])
                window = jnp.concatenate([before.astype(F32), own[:pad]], axis=0)
                fixed[k, :pad, cols] = conv_of(
                    window[pad - reach :], taps[0, :, cols], False, pad
                ).astype(BF16)
                window = jnp.concatenate([own[pad:], after.astype(F32)], axis=0)
                fixed[k, pad:, cols] = conv_of(
                    window[: pad + reach], taps[1, :, cols], True, pad
                ).astype(BF16)
        total = sum(logs[1:], logs[0])
        l1 = total.astype(BF16).astype(F32)
        l2 = (total - l1).astype(BF16).astype(F32)
        three = jnp.concatenate([l1, l2, total - l1 - l2, jnp.zeros((LOGS - 3, LANES), F32)], axis=0)
        for d in range(2):
            pack[d, size:, :] = dot(three.astype(BF16), spread[d]).astype(BF16)
            for n in range(0, channels, 256):
                cols = slice(n, n + 256)
                scale = dot(qs[...], spread[d, :, cols])
                for k in range(ring):
                    x = patched((xf, xb)[d][k], fixed, k, cols, pad, d)
                    part = slice(k * rows, (k + 1) * rows)
                    carried[part, :] = (scale[part] * x.astype(F32)).astype(BF16)
                pack[d, :size, cols] = dot(b_all[d], carried[...]).astype(BF16)

    return pl.pallas_call(
        body,
        in_specs=[smem()] + [vmem()] * (6 * ring + 2),
        out_specs=[vmem()] * 2,
        out_shape=[
            jax.ShapeDtypeStruct((2, size + LOGS, channels), BF16),
            jax.ShapeDtypeStruct((ring, 2 * pad, channels), BF16),
        ],
        scratch_shapes=[
            pltpu.VMEM((ring * rows, LANES), BF16),
            pltpu.VMEM((ring * rows, 256), BF16),
            pltpu.VMEM((2, size, ring * rows), BF16),
        ],
        compiler_params=mib(16),
        cost_estimate=pl.CostEstimate(flops=2_000_000_000, bytes_accessed=4 << 20, transcendentals=0),
        name="combine",
    )(where, *xfs, *xbs, *ends, *b_ts, *fades, *lasts, taps, spread)


def patched(x, fixed, k, cols, pad, d):
    rows = x.shape[0]
    if d == 0:
        return jnp.concatenate([fixed[k, :pad, cols], x[pad:, cols]], axis=0)
    return jnp.concatenate([x[: rows - pad, cols], fixed[k, pad:, cols]], axis=0)


def starts_of(where, xfs, xbs, fixed, b_ts, fades, lasts, spread, heads):
    ring = len(xfs)
    rows, channels = xfs[0].shape
    size = b_ts[0].shape[1]
    pad = fixed.shape[1] // 2

    def body(where, *refs):
        xf, xb, b_t, fades, lasts = (refs[i * ring : (i + 1) * ring] for i in range(5))
        fixed, spread, starts, fades_out, qs = refs[5 * ring :]
        at, logs, between = frame_logs(where, lasts, ring)
        forward = lax.broadcasted_iota(jnp.int32, logs[0].shape, 1) < heads
        fade = spread_rows(
            [jnp.where(forward, between(-1, p), between(p, ring)) for p in at], heads, spread
        )
        for d in range(2):
            fades_out[d] = fade[d]
        for k in range(ring):
            qs[k * rows : (k + 1) * rows, :] = two_parts(fades[k][...], 2 * heads)
        weights = [
            spread_rows(
                [
                    jnp.where(forward, between(at[k], at[j]), between(at[j], at[k]))
                    for k in range(ring)
                ],
                heads,
                spread,
            )
            for j in range(ring)
        ]
        for d in range(2):
            for n in range(0, channels, 256):
                cols = slice(n, n + 256)
                scale = dot(qs[...], spread[d, :, cols])
                for k in range(ring):
                    x = patched((xf, xb)[d][k], fixed, k, cols, pad, d)
                    part = slice(k * rows, (k + 1) * rows)
                    added = dot(b_t[k][d], (scale[part] * x.astype(F32)).astype(BF16))
                    for j in range(ring):
                        if j == k:
                            continue
                        before = at[k] < at[j] if d == 0 else at[k] > at[j]
                        term = jnp.where(before, weights[j][d][k : k + 1, cols], 0.0) * added
                        if k == (1 if j == 0 else 0):
                            starts[j, d, :, cols] = term
                        else:
                            starts[j, d, :, cols] += term

    return pl.pallas_call(
        body,
        in_specs=[smem()] + [vmem()] * (5 * ring + 2),
        out_specs=[vmem()] * 2,
        out_shape=[
            jax.ShapeDtypeStruct((ring, 2, size, channels), F32),
            jax.ShapeDtypeStruct((2, ring + -ring % 8, channels), F32),
        ],
        scratch_shapes=[pltpu.VMEM((ring * rows, LANES), BF16)],
        compiler_params=mib(16),
        cost_estimate=pl.CostEstimate(flops=1_200_000_000, bytes_accessed=8 << 20, transcendentals=0),
        name="starts",
    )(where, *xfs, *xbs, *b_ts, *fades, *lasts, fixed, spread)


def inside(k, xf, xb, fixed, bc, cum, cum_t, skip, heads):
    rows, channels = xf.shape
    size = bc.shape[1] // 4

    pad = fixed.shape[1] // 2

    def body(xf, xb, fixed, bc, cum, cum_t, skip, y):
        row, col = (lax.broadcasted_iota(jnp.int32, (rows, rows), d) for d in (0, 1))
        first = lax.broadcasted_iota(jnp.int32, (rows, LANES), 1) < HEAD_DIM
        scores = []
        for d in range(2):
            b_rows = bc[:, 2 * d * size : (2 * d + 1) * size]
            c_rows = bc[:, (2 * d + 1) * size : (2 * d + 2) * size]
            s = lax.dot_general(
                c_rows, b_rows, (((1,), (1,)), ((), ())), preferred_element_type=F32
            )
            scores.append(jnp.where(row >= col if d == 0 else row <= col, s, 0.0))
        for pair in range(channels // LANES):
            cols = slice(pair * LANES, (pair + 1) * LANES)
            weights = []
            for h in range(pair * (LANES // HEAD_DIM), (pair + 1) * (LANES // HEAD_DIM)):
                sides = []
                for d in range(2):
                    at = d * heads + h
                    gap = jnp.minimum(cum[:, at : at + 1] - cum_t[at : at + 1, :], 0.0)
                    dt = cum_t[2 * heads + at : 2 * heads + at + 1, :]
                    sides.append((jnp.exp2(gap) * (scores[d] * dt)).astype(BF16))
                weights.append(jnp.concatenate(sides, axis=1))
            sides = [patched(x, fixed, k, cols, pad, d) for d, x in enumerate((xf, xb))]
            x_pair = jnp.concatenate(sides, axis=0)
            out = dot(jnp.concatenate(weights, axis=0), x_pair)
            total = jnp.where(first, out[:rows], out[rows:])
            total += skip[0:1, cols] * sides[0].astype(F32)
            total += skip[1:2, cols] * sides[1].astype(F32)
            y[:, cols] = total

    return pl.pallas_call(
        body,
        in_specs=[vmem()] * 7,
        out_specs=vmem(),
        out_shape=jax.ShapeDtypeStruct((rows, channels), F32),
        compiler_params=mib(12),
        cost_estimate=pl.CostEstimate(flops=1_200_000_000, bytes_accessed=2 << 20, transcendentals=0),
        name="inside",
    )(xf, xb, fixed, bc, cum, cum_t, skip)


def gates(pieces, w_gate):
    rows, depth = sum(p.shape[0] for p in pieces), pieces[0].shape[1]
    channels, count = w_gate.shape[1], len(pieces)

    def body(*refs):
        wg, gate, block = refs[count:]
        gather(refs[:count], block)
        for n in range(0, channels, 256):
            raw = dot(block[...], wg[:, n : n + 256]).astype(BF16)
            gate[:, n : n + 256] = silu(raw.astype(F32))

    return pl.pallas_call(
        body,
        in_specs=[vmem()] * (count + 1),
        out_specs=vmem(),
        out_shape=jax.ShapeDtypeStruct((rows, channels), F32),
        scratch_shapes=[pltpu.VMEM((rows, depth), BF16)],
        compiler_params=mib(12),
        cost_estimate=pl.CostEstimate(
            flops=2 * rows * depth * channels, bytes_accessed=2 * depth * channels, transcendentals=0
        ),
        name="gates",
    )(*pieces, w_gate)


def log_rows(rows):
    rows = rows.astype(F32)
    return rows[0:1] + rows[1:2] + rows[2:3]


def messages(where, mine, theirs, groups, parts):
    size, channels = mine.shape[1] - LOGS, mine.shape[2]
    width = channels // parts

    def body(where, mine, theirs, *outs):
        group, second = where[1], where[2] == 1
        cols = pl.ds(pl.multiple_of(where[2] * width, LANES), width)
        for d in range(2):
            own, other = log_rows(mine[d, size:, cols]), log_rows(theirs[d, size:, cols])
            later = second if d == 0 else jnp.logical_not(second)
            scale_own = jnp.where(later, 1.0, jnp.exp2(other))
            scale_other = jnp.where(later, jnp.exp2(own), 1.0)
            total = own + other
            l1 = total.astype(BF16).astype(F32)
            l2 = (total - l1).astype(BF16).astype(F32)
            logs = jnp.concatenate(
                [l1, l2, total - l1 - l2, jnp.zeros((LOGS - 3, width), F32)], axis=0
            ).astype(BF16)
            state = scale_own * mine[d, :size, cols].astype(F32)
            state = (state + scale_other * theirs[d, :size, cols].astype(F32)).astype(BF16)
            for k, out in enumerate(outs, 1):
                onward = group + k < groups

                @pl.when(onward if d == 0 else jnp.logical_not(onward))
                def _(out=out):
                    out[:size, :] = state
                    out[size:, :] = logs

    return pl.pallas_call(
        body,
        in_specs=[smem(), vmem(), vmem()],
        out_specs=[vmem()] * (groups - 1),
        out_shape=[jax.ShapeDtypeStruct((size + LOGS, width), BF16)] * (groups - 1),
        compiler_params=mib(16),
        cost_estimate=pl.CostEstimate(flops=1_000_000, bytes_accessed=2 << 20, transcendentals=0),
        name="messages",
    )(where, mine, theirs)


def entering(where, received, groups):
    size, width = received[0].shape[0] - LOGS, received[0].shape[1]

    def body(where, *refs):
        got, out = refs[:-1], refs[-1]
        group = where[1]
        for d in range(2):
            log = jnp.zeros((1, width), F32)
            state = jnp.zeros((size, width), F32)
            for far in range(1, groups):
                ref = got[far - 1] if d == 0 else got[groups - far - 1]
                holds = far <= (group if d == 0 else groups - 1 - group)
                scale = jnp.where(holds, jnp.exp2(log), 0.0)
                state += scale * ref[:size, :].astype(F32)
                log = jnp.where(holds, log + log_rows(ref[size:, :]), log)
            out[d] = state.astype(BF16)

    return pl.pallas_call(
        body,
        in_specs=[smem()] + [vmem()] * len(received),
        out_specs=vmem(),
        out_shape=jax.ShapeDtypeStruct((2, size, width), BF16),
        compiler_params=mib(16),
        cost_estimate=pl.CostEstimate(flops=1_000_000, bytes_accessed=2 << 20, transcendentals=0),
        name="entering",
    )(where, *received)


SUB = 16


def pack_squares(row):
    high = row.astype(BF16).astype(F32)
    return jnp.concatenate([high, row - high, jnp.zeros((SUB - 2, LANES), F32)], axis=0).astype(BF16)


def squares_of(packed):
    v = packed.astype(F32)
    return v[0:1] + v[1:2]


def finish(where, k, y, bc, reached, gate, starts, fades, theirs, mine, other, spread, gain, w_out):
    rows, channels = y.shape
    size = bc.shape[1] // 4
    width = w_out.shape[1]
    half = rows // 2
    last = k == 0
    part = mine.shape[2]
    step = min(256, part)
    across = width // LANES
    count = half // SUB * across

    def body(where, y, bc, reached, gate, starts, fades, theirs, mine, other, spread, gain, w_out, *refs):
        outs, scaled = refs[:-1], refs[-1]
        second = where[2] == 1
        square = jnp.zeros((rows, LANES), F32)
        for n in range(0, channels, step):
            cols = slice(n, n + step)
            total = y[:, cols]
            for d in range(2):
                c_rows = bc[:, (2 * d + 1) * size : (2 * d + 2) * size]
                near = second if d == 0 else jnp.logical_not(second)
                at = slice(n % part, n % part + step)
                enter = jnp.where(where[2] == n // part, mine[d, :, at], other[d, :, at]).astype(F32)
                log = jnp.where(near, log_rows(theirs[d, size:, cols]), 0.0)
                enter = jnp.exp2(log) * enter
                enter += jnp.where(near, theirs[d, :size, cols].astype(F32), 0.0)
                state = starts[0, d, :, cols] + fades[d, k : k + 1, cols] * enter
                total += dot(reached[...], spread[d, :, cols]) * dot(c_rows, state.astype(BF16))
            gated = total * gate[:, cols]
            for t in range(0, step, LANES):
                square += gated[:, t : t + LANES] * gated[:, t : t + LANES]
            scaled[:, cols] = (gated * gain[:, cols]).astype(BF16)
        sums = jnp.broadcast_to(jnp.sum(square, axis=1, keepdims=True), (rows, LANES))
        row = sums.T[0:1, :]
        if last:
            outs[1][...] = jnp.broadcast_to(row, (SUB, rows))
        else:
            for out in outs:
                out[count] = pack_squares(row)
        for n in range(0, width, 256):
            value = dot(scaled[...], w_out[:, n : n + 256])
            if last:
                outs[0][:, n : n + 256] = value
                continue
            value = value.astype(BF16)
            for i in range(rows // SUB):
                for j in range(0, 256, LANES):
                    tile = value[i * SUB : (i + 1) * SUB, j : j + LANES]
                    place = i % (half // SUB) * across + (n + j) // LANES
                    outs[i * SUB // half][place] = tile

    if last:
        shapes = [((rows, width), F32), ((SUB, rows), F32)]
    else:
        shapes = [((count + 1, SUB, LANES), BF16)] * 2
    specs = [smem()] + [vmem()] * 12
    specs[5] = pl.BlockSpec((1,) + starts.shape[1:], lambda i: (k, 0, 0, 0))
    return pl.pallas_call(
        body,
        grid=(1,),
        in_specs=specs,
        out_specs=[vmem()] * len(shapes),
        out_shape=[jax.ShapeDtypeStruct(*s) for s in shapes],
        scratch_shapes=[pltpu.VMEM((rows, channels), BF16)],
        compiler_params=mib(16),
        cost_estimate=pl.CostEstimate(
            flops=2 * rows * channels * width, bytes_accessed=2 * channels * width, transcendentals=0
        ),
        name="finish",
    )(where, y, bc, reached, gate, starts, fades, theirs, mine, other, spread, gain, w_out)


def plus(value, got):
    count = value.shape[0] - 1

    def body(value, got, out):
        for n in range(0, count, 8):
            part = slice(n, min(n + 8, count))
            out[part] = (value[part].astype(F32) + got[part].astype(F32)).astype(BF16)
        out[count] = pack_squares(squares_of(value[count]) + squares_of(got[count]))

    return pl.pallas_call(
        body,
        in_specs=[vmem()] * 2,
        out_specs=vmem(),
        out_shape=jax.ShapeDtypeStruct(value.shape, BF16),
        compiler_params=mib(8),
        name="plus",
    )(value, got)


def normalize(value, square, halves, channels):
    rows, width = value.shape
    half = rows // 2
    across = width // LANES
    count = half // SUB * across
    each = [len(h) for h in halves]

    def body(value, square, *refs):
        ins, out = refs[:-1], refs[-1]
        lane = lax.broadcasted_iota(jnp.int32, (1, rows), 1)
        groups = (ins[: each[0]], ins[each[0] :])
        sums = square[0:1, :]
        for i, group in enumerate(groups):
            for ref in group:
                got = squares_of(ref[count])
                sums = sums + jnp.where((lane >= half) == (i == 1), got, 0.0)
        scale = lax.rsqrt(sums / channels + 1e-05)
        scale = jnp.broadcast_to(scale, (LANES, rows)).T
        for i in range(rows // SUB):
            group = groups[i * SUB // half]
            for j in range(across):
                at = (slice(i * SUB, (i + 1) * SUB), slice(j * LANES, (j + 1) * LANES))
                total = value[at]
                for ref in group:
                    total = total + ref[i % (half // SUB) * across + j].astype(F32)
                out[at] = (total * scale[at[0], :]).astype(BF16)

    return pl.pallas_call(
        body,
        in_specs=[vmem()] * (2 + sum(each)),
        out_specs=vmem(),
        out_shape=jax.ShapeDtypeStruct(value.shape, BF16),
        compiler_params=mib(8),
        name="normalize",
    )(value, square, *halves[0], *halves[1])


def ring_pairs(count, step):
    return [(i, (i + step) % count) for i in range(count)]


def layer(
    tokens,
    w_gate,
    w_value,
    w_state_proj,
    w_step,
    step_bias,
    decay_rate,
    conv_taps,
    skip_gain,
    norm_gain,
    w_out,
):
    ring, frames = lax.axis_size("row"), lax.axis_size("frame")
    row, frame = lax.axis_index("row"), lax.axis_index("frame")
    channels, heads = w_gate.shape[1], step_bias.shape[1]
    span = 2 if frames % 2 == 0 else 1
    groups = frames // span
    where = jnp.stack([row, frame // span, frame % span]).astype(jnp.int32)
    own = tokens.reshape(-1, tokens.shape[2])
    far = ring // 2
    edge = 8
    end = ring - 1

    def up(v):
        return lax.ppermute(v, "row", ring_pairs(ring, 1))

    def down(v):
        return lax.ppermute(v, "row", ring_pairs(ring, -1))

    first, second, outer = split(where, own, ring, edge)
    pieces = {0: [first, second]}
    order = [0]
    from_below, from_above = [first, second], [second, first]
    for hop in range(1, far + 1):
        a, c = up(from_below[0]), down(from_above[0])
        if 2 * hop == ring:
            pieces[hop] = [a, c]
            order.append(hop)
        else:
            b, d = up(from_below[1]), down(from_above[1])
            from_below, from_above = [a, b], [c, d]
            pieces[ring - hop], pieces[hop] = [a, b], [d, c]
            order += [ring - hop, hop]
    bounds = []
    for j in range(ring):
        pairs = [(f * ring + end, (f + 1) * ring + (end + j) % ring) for f in range(frames - 1)]
        pairs += [((f + 1) * ring, f * ring + j) for f in range(frames - 1)]
        bounds.append(lax.ppermute(outer, ("frame", "row"), pairs))

    steps = jnp.swapaxes(w_step, 1, 2).reshape(-1, w_step.shape[1])
    spread, small_rows, skip = prepare(step_bias, decay_rate, skip_gain, channels)
    gain = norm_gain.reshape(1, -1)

    blocks = {}
    for k in order:
        blocks[k] = block_states(
            pieces[k],
            bounds if k == 1 else [],
            where,
            w_value,
            w_state_proj,
            steps,
            conv_taps,
            small_rows,
            heads,
        )
    xfs, xbs, ends, bcs, b_ts, cums, cum_ts, reached, fading, lasts = (
        [blocks[k][i] for k in range(ring)] for i in range(len(blocks[0]))
    )
    pack, fixed = combine(where, xfs, xbs, ends, b_ts, fading, lasts, conv_taps, spread, heads)

    if span == 2:
        swap = [(i, i ^ 1) for i in range(frames)]
        theirs = lax.ppermute(pack, "frame", swap)
    else:
        theirs = jnp.zeros_like(pack)
    received = []
    if groups > 1:
        sends = messages(where, pack, theirs, groups, span)
        for k in sorted(range(1, groups), key=lambda k: k % 2 == 0):
            pairs = [
                (g * span + s, (g + k) % groups * span + s) for g in range(groups) for s in range(span)
            ]
            received.append((k, lax.ppermute(sends[k - 1], "frame", pairs)))
        received = [v for _, v in sorted(received, key=lambda kv: kv[0])]
        enter = entering(where, received, groups)
    else:
        enter = jnp.zeros((2, pack.shape[1] - LOGS, channels // span), BF16)
    other = lax.ppermute(enter, "frame", swap) if span == 2 else enter
    inner, gate = {}, {}
    for k in order:
        inner[k] = inside(k, xfs[k], xbs[k], fixed, bcs[k], cums[k], cum_ts[k], skip, heads)
        gate[k] = gates(pieces[k], w_gate)
    starts, fades = starts_of(where, xfs, xbs, fixed, b_ts, fading, lasts, spread, heads)

    def block(k):
        return finish(
            where,
            k,
            inner[k],
            bcs[k],
            reached[k],
            gate[k],
            starts,
            fades,
            theirs,
            enter,
            other,
            spread,
            gain,
            w_out,
        )

    up_a = up_b = down_a = down_b = None
    for hop in range(far, 0, -1):
        if 2 * hop == ring:
            a, b = block(hop)
            up_a, down_b = up(a), down(b)
            continue
        (above_a, above_b), (below_a, below_b) = block(hop), block(ring - hop)
        up_b = up(above_b if up_b is None else plus(above_b, up_b))
        down_a = down(below_a if down_a is None else plus(below_a, down_a))
        up_a = up(above_a if up_a is None else plus(above_a, up_a))
        down_b = down(below_b if down_b is None else plus(below_b, down_b))
    value, square = block(0)
    halves = [[v for v in pair if v is not None] for pair in ((up_a, down_a), (up_b, down_b))]
    return normalize(value, square, halves, channels * ring).reshape(tokens.shape)


def solution(mesh):
    return jax.shard_map(
        layer,
        mesh=mesh,
        in_specs=(
            P("frame", "row", None),
            P(None, "row"),
            P(None, "row"),
            P(),
            P(None, None, "row"),
            P(None, "row"),
            P(None, "row"),
            P(None, None, "row"),
            P(None, "row"),
            P("row"),
            P("row", None),
        ),
        out_specs=P("frame", "row", None),
        check_vma=False,
    )
```

profile of v0, /device:TPU:0, one launch (start us, length us, event | category | flops | bytes accessed | tf_op | source)
XLA Modules:
  0.0 110.7 jit_solution(1246171949085265938)
XLA Ops:
  0.0 0.1 pad_add_fusion.where
  0.1 1.0 copy-done.10
  1.1 0.0 copy-start.3
  1.1 0.0 copy-start.4
  1.2 0.0 copy-start.5
  1.2 0.6 split.1
  1.8 3.1 %collective-permute-start.6 = (bf16[64,2048]{1,0:T(8,128)(2,1)S(1)}, bf16[64,2048]{1,0:T(8,128)(2,1)S(1)}, u32[]{:S(2)}, u32[]{:S(2)}) collective-permute-start(bf16[64,2048]{1,0:T(8,128)(2,1)S(1)} %get-tuple-element.66.refs_0_), channel_id=1, source_target_pairs={{0,1},{1,2},{2,3},{3,0},{4,5},{5,6},{6,7},{7,4},{8,9},{9,10},{10,1... | collective-permute-start | bytes 786440 | tf_op jit(solution)/shard_map/ppermute | solution.py:715
  4.9 2.1 %collective-permute-start.1 = (bf16[64,2048]{1,0:T(8,128)(2,1)S(1)}, bf16[64,2048]{1,0:T(8,128)(2,1)S(1)}, u32[]{:S(2)}, u32[]{:S(2)}) collective-permute-start(bf16[64,2048]{1,0:T(8,128)(2,1)S(1)} %get-tuple-element.67.refs_1_), channel_id=1, source_target_pairs={{0,3},{1,0},{2,1},{3,2},{4,7},{5,4},{6,5},{7,6},{8,11},{9,8},{10,9... | collective-permute-start | bytes 786440 | tf_op jit(solution)/shard_map/ppermute | solution.py:718
  7.0 1.3 %collective-permute-start.2 = (bf16[8,2048]{1,0:T(8,128)(2,1)S(1)}, bf16[8,2048]{1,0:T(8,128)(2,1)S(1)}, u32[]{:S(2)}, u32[]{:S(2)}) collective-permute-start(bf16[8,2048]{1,0:T(8,128)(2,1)S(1)} %get-tuple-element.71), channel_id=1, source_target_pairs={{3,7},{7,11},{11,15},{15,19},{19,23},{23,27},{27,31},{4,0},{8,4},{... | collective-permute-start | bytes 98312 | tf_op jit(solution)/shard_map/ppermute | solution.py:738
  8.2 3.9 %collective-permute-start = (bf16[64,2048]{1,0:T(8,128)(2,1)S(1)}, bf16[64,2048]{1,0:T(8,128)(2,1)S(1)}, u32[]{:S(2)}, u32[]{:S(2)}) collective-permute-start(bf16[64,2048]{1,0:T(8,128)(2,1)S(1)} %get-tuple-element.66.refs_0_), channel_id=1, source_target_pairs={{0,3},{1,0},{2,1},{3,2},{4,7},{5,4},{6,5},{7,6},{8,11},{9,8},{10,9... | collective-permute-start | bytes 786440 | tf_op jit(solution)/shard_map/ppermute | solution.py:718
  12.1 0.2 prepare.1
  12.3 0.7 collective-permute-start.3
  13.0 1.1 %collective-permute-done.6.refs_0_ = bf16[64,2048]{1,0:T(8,128)(2,1)S(1)} collective-permute-done((bf16[64,2048]{1,0:T(8,128)(2,1)S(1)}, bf16[64,2048]{1,0:T(8,128)(2,1)S(1)}, u32[]{:S(2)}, u32[]{:S(2)}) %collective-permute-start.6) | collective-permute-done | bytes 262176 | tf_op jit(solution)/shard_map/ppermute | solution.py:715
  14.1 4.2 %collective-permute-start.7 = (bf16[64,2048]{1,0:T(8,128)(2,1)S(1)}, bf16[64,2048]{1,0:T(8,128)(2,1)S(1)}, u32[]{:S(2)}, u32[]{:S(2)}) collective-permute-start(bf16[64,2048]{1,0:T(8,128)(2,1)S(1)} %collective-permute-done.6.refs_0_), channel_id=1, source_target_pairs={{0,1},{1,2},{2,3},{3,0},{4,5},{5,6},{6,7},{7,4},{8,9},{9,10},{10,1... | collective-permute-start | bytes 786440 | tf_op jit(solution)/shard_map/ppermute | solution.py:715
  18.3 1.5 %collective-permute-done.1.refs_1_ = bf16[64,2048]{1,0:T(8,128)(2,1)S(1)} collective-permute-done((bf16[64,2048]{1,0:T(8,128)(2,1)S(1)}, bf16[64,2048]{1,0:T(8,128)(2,1)S(1)}, u32[]{:S(2)}, u32[]{:S(2)}) %collective-permute-start.1) | collective-permute-done | bytes 262176 | tf_op jit(solution)/shard_map/ppermute | solution.py:718
  19.8 1.9 %collective-permute-start.8 = (bf16[64,2048]{1,0:T(8,128)(2,1)S(1)}, bf16[64,2048]{1,0:T(8,128)(2,1)S(1)}, u32[]{:S(2)}, u32[]{:S(2)}) collective-permute-start(bf16[64,2048]{1,0:T(8,128)(2,1)S(1)} %collective-permute-done.1.refs_1_), channel_id=1, source_target_pairs={{0,3},{1,0},{2,1},{3,2},{4,7},{5,4},{6,5},{7,6},{8,11},{9,8},{10,9... | collective-permute-start | bytes 786440 | tf_op jit(solution)/shard_map/ppermute | solution.py:718
  21.7 3.1 %block_states.4 = (bf16[128,1024]{1,0:T(8,128)(2,1)S(1)}, bf16[128,1024]{1,0:T(8,128)(2,1)S(1)}, bf16[16,1024]{1,0:T(8,128)(2,1)S(1)}, bf16[128,512]{1,0:T(8,128...) custom-call(s32[3]{0:T(128)S(1)} %pad_add_fusion.where, ...), custom_call_target="tpu_custom_call" | custom-call | flops 1308622848 | bytes 6815744 | tf_op jit(solution)/shard_map/block_states/pallas_call | solution.py:226
  24.8 0.7 collective-permute-start.4
  25.5 0.7 collective-permute-start.5
  26.2 3.1 %block_states.7 = (bf16[128,1024]{1,0:T(8,128)(2,1)S(1)}, bf16[128,1024]{1,0:T(8,128)(2,1)S(1)}, bf16[16,1024]{1,0:T(8,128)(2,1)S(1)}, bf16[128,512]{1,0:T(8,128...) custom-call(s32[3]{0:T(128)S(1)} %pad_add_fusion.where, ...), custom_call_target="tpu_custom_call" | custom-call | flops 1308622848 | bytes 6815744 | tf_op jit(solution)/shard_map/block_states/pallas_call | solution.py:226
  29.2 1.8 %collective-permute-done.refs_0_ = bf16[64,2048]{1,0:T(8,128)(2,1)S(1)} collective-permute-done((bf16[64,2048]{1,0:T(8,128)(2,1)S(1)}, bf16[64,2048]{1,0:T(8,128)(2,1)S(1)}, u32[]{:S(2)}, u32[]{:S(2)}) %collective-permute-start) | collective-permute-done | bytes 262176 | tf_op jit(solution)/shard_map/ppermute | solution.py:718
  31.0 3.4 %block_states.5 = (bf16[128,1024]{1,0:T(8,128)(2,1)S(1)}, bf16[128,1024]{1,0:T(8,128)(2,1)S(1)}, bf16[32,1024]{1,0:T(8,128)(2,1)S(1)}, bf16[128,512]{1,0:T(8,128...) custom-call(s32[3]{0:T(128)S(1)} %pad_add_fusion.where, ...), custom_call_target="tpu_custom_call" | custom-call | flops 1472200704 | bytes 6815744 | tf_op jit(solution)/shard_map/block_states/pallas_call | solution.py:226
  34.5 2.9 %collective-permute-done.7.refs_0_ = bf16[64,2048]{1,0:T(8,128)(2,1)S(1)} collective-permute-done((bf16[64,2048]{1,0:T(8,128)(2,1)S(1)}, bf16[64,2048]{1,0:T(8,128)(2,1)S(1)}, u32[]{:S(2)}, u32[]{:S(2)}) %collective-permute-start.7) | collective-permute-done | bytes 262176 | tf_op jit(solution)/shard_map/ppermute | solution.py:715
  37.4 4.1 %collective-permute-done.8.refs_1_ = bf16[64,2048]{1,0:T(8,128)(2,1)S(1)} collective-permute-done((bf16[64,2048]{1,0:T(8,128)(2,1)S(1)}, bf16[64,2048]{1,0:T(8,128)(2,1)S(1)}, u32[]{:S(2)}, u32[]{:S(2)}) %collective-permute-start.8) | collective-permute-done | bytes 262176 | tf_op jit(solution)/shard_map/ppermute | solution.py:718
  41.4 3.1 %block_states.6 = (bf16[128,1024]{1,0:T(8,128)(2,1)S(1)}, bf16[128,1024]{1,0:T(8,128)(2,1)S(1)}, bf16[16,1024]{1,0:T(8,128)(2,1)S(1)}, bf16[128,512]{1,0:T(8,128...) custom-call(s32[3]{0:T(128)S(1)} %pad_add_fusion.where, ...), custom_call_target="tpu_custom_call" | custom-call | flops 1308622848 | bytes 6815744 | tf_op jit(solution)/shard_map/block_states/pallas_call | solution.py:226
  44.5 3.0 %combine.1 = (bf16[2,136,1024]{2,1,0:T(8,128)(2,1)S(1)}, bf16[4,16,1024]{2,1,0:T(8,128)(2,1)S(1)}) custom-call(s32[3]{0:T(128)S(1)} %pad_add_fusion.where, bf16[128,1024]{1,0:T(8,128)(2,1)S(1)} %get-tuple-element.69.refs_0_.xf, bf16[128,1024]{1,0:T(8,128)(2,1)S(1)} %get-tuple-element.72.refs_1_.xf, bf16[128,1024]{1,0:T(8,128)(2,1)S(1)} %get-tuple-element.73.refs_2_.xf, ...), custom_call_target="tpu_custom_call" | custom-call | flops 2000000000 | bytes 4194304 | tf_op jit(solution)/shard_map/combine/pallas_call | solution.py:313
  47.5 3.6 %collective-permute-start.10 = (bf16[2,136,1024]{2,1,0:T(8,128)(2,1)S(1)}, bf16[2,136,1024]{2,1,0:T(8,128)(2,1)S(1)}, u32[]{:S(2)}, u32[]{:S(2)}) collective-permute-start(bf16[2,136,1024]{2,1,0:T(8,128)(2,1)S(1)} %get-tuple-element.103.mine), channel_id=1, source_target_pairs={{0,4},{4,0},{8,12},{12,8},{16,20},{20,16},{24,28},{28,24},{1,5},{5... | collective-permute-start | bytes 1671176 | tf_op jit(solution)/shard_map/ppermute | solution.py:764
  51.1 1.6 %collective-permute-done.10.theirs = bf16[2,136,1024]{2,1,0:T(8,128)(2,1)S(1)} collective-permute-done((bf16[2,136,1024]{2,1,0:T(8,128)(2,1)S(1)}, bf16[2,136,1024]{2,1,0:T(8,128)(2,1)S(1)}, u32[]{:S(2)}, u32[]{:S(2)}) %collective-permute-start.10) | collective-permute-done | bytes 557088 | tf_op jit(solution)/shard_map/ppermute | solution.py:764
  52.7 0.7 messages.1
  53.4 1.5 %collective-permute-start.11 = (bf16[136,512]{1,0:T(8,128)(2,1)S(1)}, bf16[136,512]{1,0:T(8,128)(2,1)S(1)}, u32[]{:S(2)}, u32[]{:S(2)}) collective-permute-start(bf16[136,512]{1,0:T(8,128)(2,1)S(1)} %get-tuple-element.104), channel_id=1, source_target_pairs={{0,8},{4,12},{8,16},{12,20},{16,24},{20,28},{24,0},{28,4},{1,9},{5... | collective-permute-start | bytes 417800 | tf_op jit(solution)/shard_map/ppermute | solution.py:774
  54.9 1.2 %collective-permute-start.12 = (bf16[136,512]{1,0:T(8,128)(2,1)S(1)}, bf16[136,512]{1,0:T(8,128)(2,1)S(1)}, u32[]{:S(2)}, u32[]{:S(2)}) collective-permute-start(bf16[136,512]{1,0:T(8,128)(2,1)S(1)} %get-tuple-element.105), channel_id=1, source_target_pairs={{0,16},{4,20},{8,24},{12,28},{16,0},{20,4},{24,8},{28,12},{1,17},{... | collective-permute-start | bytes 417800 | tf_op jit(solution)/shard_map/ppermute | solution.py:774
  56.1 1.8 %collective-permute-start.13 = (bf16[136,512]{1,0:T(8,128)(2,1)S(1)}, bf16[136,512]{1,0:T(8,128)(2,1)S(1)}, u32[]{:S(2)}, u32[]{:S(2)}) collective-permute-start(bf16[136,512]{1,0:T(8,128)(2,1)S(1)} %get-tuple-element.106), channel_id=1, source_target_pairs={{0,24},{4,28},{8,0},{12,4},{16,8},{20,12},{24,16},{28,20},{1,25},{... | collective-permute-start | bytes 417800 | tf_op jit(solution)/shard_map/ppermute | solution.py:774
  57.9 0.8 gates.5.gate
  58.7 0.8 gates.7.gate
  59.6 1.4 %collective-permute-done.11.refs_0_ = bf16[136,512]{1,0:T(8,128)(2,1)S(1)} collective-permute-done((bf16[136,512]{1,0:T(8,128)(2,1)S(1)}, bf16[136,512]{1,0:T(8,128)(2,1)S(1)}, u32[]{:S(2)}, u32[]{:S(2)}) %collective-permute-start.11) | collective-permute-done | bytes 139296 | tf_op jit(solution)/shard_map/ppermute | solution.py:774
  60.9 2.3 %collective-permute-done.12.refs_1_ = bf16[136,512]{1,0:T(8,128)(2,1)S(1)} collective-permute-done((bf16[136,512]{1,0:T(8,128)(2,1)S(1)}, bf16[136,512]{1,0:T(8,128)(2,1)S(1)}, u32[]{:S(2)}, u32[]{:S(2)}) %collective-permute-start.12) | collective-permute-done | bytes 139296 | tf_op jit(solution)/shard_map/ppermute | solution.py:774
  63.3 0.1 collective-permute-done.13.refs_2_
  63.4 0.7 entering.1.mine
  64.1 0.1 collective-permute-start.14
  64.2 0.8 gates.6.gate
  65.0 0.0 copy-start.2
  65.0 0.0 copy-start.6
  65.0 2.7 %starts.1 = (f32[4,2,128,1024]{3,2,1,0:T(8,128)S(1)}, f32[2,8,1024]{2,1,0:T(8,128)S(1)}) custom-call(s32[3]{0:T(128)S(1)} %pad_add_fusion.where, bf16[128,1024]{1,0:T(8,128)(2,1)S(1)} %get-tuple-element.69.refs_0_.xf, bf16[128,1024]{1,0:T(8,128)(2,1)S(1)} %get-tuple-element.72.refs_1_.xf, bf16[128,1024]{1,0:T(8,128)(2,1)S(1)} %get-tuple-element.73.refs_2_.xf, ...), custom_call_target="tpu_custom_call" | custom-call | flops 1200000000 | bytes 8388608 | tf_op jit(solution)/shard_map/starts/pallas_call | solution.py:386
  67.8 0.9 inside.6.y
  68.7 1.8 %finish.6 = (bf16[65,16,128]{2,1,0:T(8,128)(2,1)S(1)}, bf16[65,16,128]{2,1,0:T(8,128)(2,1)S(1)}) custom-call(s32[3]{0:T(128)S(1)} %pad_add_fusion.where, f32[128,1024]{1,0:T(8,128)S(1)} %inside.6.y, bf16[128,512]{1,0:T(8,128)(2,1)S(1)} %get-tuple-element.114.bc, bf16[128,128]{1,0:T(8,128)(2,1)S(1)} %get-tuple-element.117.reached, ...), custom_call_target="tpu_custom_call" | custom-call | flops 536870912 | bytes 4194304 | tf_op jit(solution)/shard_map/finish/pallas_call | solution.py:615
  70.5 2.2 %collective-permute-start.15 = (bf16[65,16,128]{2,1,0:T(8,128)(2,1)S(1)}, bf16[65,16,128]{2,1,0:T(8,128)(2,1)S(1)}, u32[]{:S(2)}, u32[]{:S(2)}) collective-permute-start(bf16[65,16,128]{2,1,0:T(8,128)(2,1)S(1)} %get-tuple-element.118), channel_id=1, source_target_pairs={{0,1},{1,2},{2,3},{3,0},{4,5},{5,6},{6,7},{7,4},{8,9},{9,10},{10,1... | collective-permute-start | bytes 798728 | tf_op jit(solution)/shard_map/ppermute | solution.py:715
  72.6 2.3 %collective-permute-start.19 = (bf16[65,16,128]{2,1,0:T(8,128)(2,1)S(1)}, bf16[65,16,128]{2,1,0:T(8,128)(2,1)S(1)}, u32[]{:S(2)}, u32[]{:S(2)}) collective-permute-start(bf16[65,16,128]{2,1,0:T(8,128)(2,1)S(1)} %get-tuple-element.126), channel_id=1, source_target_pairs={{0,3},{1,0},{2,1},{3,2},{4,7},{5,4},{6,5},{7,6},{8,11},{9,8},{10,9... | collective-permute-start | bytes 798728 | tf_op jit(solution)/shard_map/ppermute | solution.py:718
  74.9 0.9 inside.5.y
  75.8 0.9 inside.7.y
  76.7 1.8 %finish.7 = (bf16[65,16,128]{2,1,0:T(8,128)(2,1)S(1)}, bf16[65,16,128]{2,1,0:T(8,128)(2,1)S(1)}) custom-call(s32[3]{0:T(128)S(1)} %pad_add_fusion.where, f32[128,1024]{1,0:T(8,128)S(1)} %inside.7.y, bf16[128,512]{1,0:T(8,128)(2,1)S(1)} %get-tuple-element.119.bc, bf16[128,128]{1,0:T(8,128)(2,1)S(1)} %get-tuple-element.122.reached, ...), custom_call_target="tpu_custom_call" | custom-call | flops 536870912 | bytes 4194304 | tf_op jit(solution)/shard_map/finish/pallas_call | solution.py:615
  78.5 2.0 %collective-permute-start.17 = (bf16[65,16,128]{2,1,0:T(8,128)(2,1)S(1)}, bf16[65,16,128]{2,1,0:T(8,128)(2,1)S(1)}, u32[]{:S(2)}, u32[]{:S(2)}) collective-permute-start(bf16[65,16,128]{2,1,0:T(8,128)(2,1)S(1)} %get-tuple-element.123), channel_id=1, source_target_pairs={{0,3},{1,0},{2,1},{3,2},{4,7},{5,4},{6,5},{7,6},{8,11},{9,8},{10,9... | collective-permute-start | bytes 798728 | tf_op jit(solution)/shard_map/ppermute | solution.py:718
  80.5 1.8 %finish.5 = (bf16[65,16,128]{2,1,0:T(8,128)(2,1)S(1)}, bf16[65,16,128]{2,1,0:T(8,128)(2,1)S(1)}) custom-call(s32[3]{0:T(128)S(1)} %pad_add_fusion.where, f32[128,1024]{1,0:T(8,128)S(1)} %inside.5.y, bf16[128,512]{1,0:T(8,128)(2,1)S(1)} %get-tuple-element.109.bc, bf16[128,128]{1,0:T(8,128)(2,1)S(1)} %get-tuple-element.112.reached, ...), custom_call_target="tpu_custom_call" | custom-call | flops 536870912 | bytes 4194304 | tf_op jit(solution)/shard_map/finish/pallas_call | solution.py:615
  82.3 0.1 collective-permute-start.18
  82.4 0.1 plus.2
  82.5 0.1 collective-permute-start.16
  82.5 5.1 %collective-permute-done.19.got = bf16[65,16,128]{2,1,0:T(8,128)(2,1)S(1)} collective-permute-done((bf16[65,16,128]{2,1,0:T(8,128)(2,1)S(1)}, bf16[65,16,128]{2,1,0:T(8,128)(2,1)S(1)}, u32[]{:S(2)}, u32[]{:S(2)}) %collective-permute-start.19) | collective-permute-done | bytes 266272 | tf_op jit(solution)/shard_map/ppermute | solution.py:718
  87.6 0.1 plus.3
  87.7 8.2 %collective-permute-start.20 = (bf16[65,16,128]{2,1,0:T(8,128)(2,1)S(1)}, bf16[65,16,128]{2,1,0:T(8,128)(2,1)S(1)}, u32[]{:S(2)}, u32[]{:S(2)}) collective-permute-start(bf16[65,16,128]{2,1,0:T(8,128)(2,1)S(1)} %plus.3), channel_id=1, source_target_pairs={{0,3},{1,0},{2,1},{3,2},{4,7},{5,4},{6,5},{7,6},{8,11},{9,8},{10,9... | collective-permute-start | bytes 798728 | tf_op jit(solution)/shard_map/ppermute | solution.py:718
  95.9 0.8 gates.4.gate
  96.7 0.9 inside.4.y
  97.6 1.8 %finish.4 = (f32[128,2048]{1,0:T(8,128)S(1)}, f32[16,128]{1,0:T(8,128)S(1)}) custom-call(s32[3]{0:T(128)S(1)} %pad_add_fusion.where, f32[128,1024]{1,0:T(8,128)S(1)} %inside.4.y, bf16[128,512]{1,0:T(8,128)(2,1)S(1)} %get-tuple-element.96.bc, bf16[128,128]{1,0:T(8,128)(2,1)S(1)} %get-tuple-element.100.reached, f32[128,1024]{1,0:T(8,128)S(1)} %gates.4.gate, ...), custom_call_target="tpu_custom_call" | custom-call | flops 536870912 | bytes 4194304 | tf_op jit(solution)/shard_map/finish/pallas_call | solution.py:615
  99.4 5.6 %collective-permute-done.16.refs_0_ = bf16[65,16,128]{2,1,0:T(8,128)(2,1)S(1)} collective-permute-done((bf16[65,16,128]{2,1,0:T(8,128)(2,1)S(1)}, bf16[65,16,128]{2,1,0:T(8,128)(2,1)S(1)}, u32[]{:S(2)}, u32[]{:S(2)}) %collective-permute-start.16) | collective-permute-done | bytes 266272 | tf_op jit(solution)/shard_map/ppermute | solution.py:715
  105.0 4.7 %collective-permute-done.20.refs_3_ = bf16[65,16,128]{2,1,0:T(8,128)(2,1)S(1)} collective-permute-done((bf16[65,16,128]{2,1,0:T(8,128)(2,1)S(1)}, bf16[65,16,128]{2,1,0:T(8,128)(2,1)S(1)}, u32[]{:S(2)}, u32[]{:S(2)}) %collective-permute-start.20) | collective-permute-done | bytes 266272 | tf_op jit(solution)/shard_map/ppermute | solution.py:718
  109.7 1.0 normalize.1
  (26 shorter events, 0.1 us)
Async XLA Ops:
  0.1 1.0 copy-start.10
  1.1 11.0 %copy-start.7 = (f32[2,16]{1,0:T(2,128)S(1)}, f32[2,16]{1,0:T(2,128)}, u32[]{:S(2)}) copy-start(f32[2,16]{1,0:T(2,128)} %bias.1) | copy-start | bytes 388
  1.1 11.0 %copy-start.8 = (f32[2,16]{1,0:T(2,128)S(1)}, f32[2,16]{1,0:T(2,128)}, u32[]{:S(2)}) copy-start(f32[2,16]{1,0:T(2,128)} %rate.1) | copy-start | bytes 388
  1.1 11.0 %copy-start.9 = (f32[2,16]{1,0:T(2,128)S(1)}, f32[2,16]{1,0:T(2,128)}, u32[]{:S(2)}) copy-start(f32[2,16]{1,0:T(2,128)} %skip.1) | copy-start | bytes 388
  1.1 20.6 %copy-start.1 = (bf16[2048,1024]{1,0:T(8,128)(2,1)S(1)}, bf16[2048,1024]{1,0:T(8,128)(2,1)}, u32[]{:S(2)}) copy-start(bf16[2048,1024]{1,0:T(8,128)(2,1)} %refs_2_.9) | copy-start | bytes 12582916
  1.1 20.6 %copy-start.3 = (bf16[2048,512]{1,0:T(8,128)(2,1)S(1)}, bf16[2048,512]{1,0:T(8,128)(2,1)}, u32[]{:S(2)}) copy-start(bf16[2048,512]{1,0:T(8,128)(2,1)} %refs_3_.5) | copy-start | bytes 6291460
  1.1 20.6 %copy-start.4 = (bf16[2,2048,16]{1,2,0:T(8,128)(2,1)S(1)}, bf16[2,2048,16]{1,2,0:T(8,128)(2,1)}, u32[]{:S(2)}) copy-start(bf16[2,2048,16]{1,2,0:T(8,128)(2,1)} %param.15) | copy-start | bytes 393220
  1.2 20.5 %copy-start.5 = (f32[2,4,1024]{2,1,0:T(4,128)S(1)}, f32[2,4,1024]{2,1,0:T(4,128)}, u32[]{:S(2)}) copy-start(f32[2,4,1024]{2,1,0:T(4,128)} %refs_24_.1) | copy-start | bytes 98308
  1.8 12.3 %collective-permute-start.6 = (bf16[64,2048]{1,0:T(8,128)(2,1)S(1)}, bf16[64,2048]{1,0:T(8,128)(2,1)S(1)}, u32[]{:S(2)}, u32[]{:S(2)}) collective-permute-start(bf16[64,2048]{1,0:T(8,128)(2,1)S(1)} %get-tuple-element.66.refs_0_), channel_id=1, source_target_pairs={{0,1},{1,2},{2,3},{3,0},{4,5},{5,6},{6,7},{7,4},{8,9},{9,10},{10,1... | collective-permute-start | bytes 786440 | tf_op jit(solution)/shard_map/ppermute | solution.py:715
  4.9 14.9 %collective-permute-start.1 = (bf16[64,2048]{1,0:T(8,128)(2,1)S(1)}, bf16[64,2048]{1,0:T(8,128)(2,1)S(1)}, u32[]{:S(2)}, u32[]{:S(2)}) collective-permute-start(bf16[64,2048]{1,0:T(8,128)(2,1)S(1)} %get-tuple-element.67.refs_1_), channel_id=1, source_target_pairs={{0,3},{1,0},{2,1},{3,2},{4,7},{5,4},{6,5},{7,6},{8,11},{9,8},{10,9... | collective-permute-start | bytes 786440 | tf_op jit(solution)/shard_map/ppermute | solution.py:718
  7.0 18.5 %collective-permute-start.9 = (bf16[64,2048]{1,0:T(8,128)(2,1)S(1)}, bf16[64,2048]{1,0:T(8,128)(2,1)S(1)}, u32[]{:S(2)}, u32[]{:S(2)}) collective-permute-start(bf16[64,2048]{1,0:T(8,128)(2,1)S(1)} %get-tuple-element.67.refs_1_), channel_id=1, source_target_pairs={{0,1},{1,2},{2,3},{3,0},{4,5},{5,6},{6,7},{7,4},{8,9},{9,10},{10,1... | collective-permute-start | bytes 786440 | tf_op jit(solution)/shard_map/ppermute | solution.py:715
  7.0 5.4 %collective-permute-start.2 = (bf16[8,2048]{1,0:T(8,128)(2,1)S(1)}, bf16[8,2048]{1,0:T(8,128)(2,1)S(1)}, u32[]{:S(2)}, u32[]{:S(2)}) collective-permute-start(bf16[8,2048]{1,0:T(8,128)(2,1)S(1)} %get-tuple-element.71), channel_id=1, source_target_pairs={{3,7},{7,11},{11,15},{15,19},{19,23},{23,27},{27,31},{4,0},{8,4},{... | collective-permute-start | bytes 98312 | tf_op jit(solution)/shard_map/ppermute | solution.py:738
  8.2 22.8 %collective-permute-start = (bf16[64,2048]{1,0:T(8,128)(2,1)S(1)}, bf16[64,2048]{1,0:T(8,128)(2,1)S(1)}, u32[]{:S(2)}, u32[]{:S(2)}) collective-permute-start(bf16[64,2048]{1,0:T(8,128)(2,1)S(1)} %get-tuple-element.66.refs_0_), channel_id=1, source_target_pairs={{0,3},{1,0},{2,1},{3,2},{4,7},{5,4},{6,5},{7,6},{8,11},{9,8},{10,9... | collective-permute-start | bytes 786440 | tf_op jit(solution)/shard_map/ppermute | solution.py:718
  12.3 12.5 %collective-permute-start.3 = (bf16[8,2048]{1,0:T(8,128)(2,1)S(1)}, bf16[8,2048]{1,0:T(8,128)(2,1)S(1)}, u32[]{:S(2)}, u32[]{:S(2)}) collective-permute-start(bf16[8,2048]{1,0:T(8,128)(2,1)S(1)} %get-tuple-element.71), channel_id=1, source_target_pairs={{3,4},{7,8},{11,12},{15,16},{19,20},{23,24},{27,28},{4,1},{8,5},{1... | collective-permute-start | bytes 98312 | tf_op jit(solution)/shard_map/ppermute | solution.py:738
  14.1 23.3 %collective-permute-start.7 = (bf16[64,2048]{1,0:T(8,128)(2,1)S(1)}, bf16[64,2048]{1,0:T(8,128)(2,1)S(1)}, u32[]{:S(2)}, u32[]{:S(2)}) collective-permute-start(bf16[64,2048]{1,0:T(8,128)(2,1)S(1)} %collective-permute-done.6.refs_0_), channel_id=1, source_target_pairs={{0,1},{1,2},{2,3},{3,0},{4,5},{5,6},{6,7},{7,4},{8,9},{9,10},{10,1... | collective-permute-start | bytes 786440 | tf_op jit(solution)/shard_map/ppermute | solution.py:715
  19.8 21.6 %collective-permute-start.8 = (bf16[64,2048]{1,0:T(8,128)(2,1)S(1)}, bf16[64,2048]{1,0:T(8,128)(2,1)S(1)}, u32[]{:S(2)}, u32[]{:S(2)}) collective-permute-start(bf16[64,2048]{1,0:T(8,128)(2,1)S(1)} %collective-permute-done.1.refs_1_), channel_id=1, source_target_pairs={{0,3},{1,0},{2,1},{3,2},{4,7},{5,4},{6,5},{7,6},{8,11},{9,8},{10,9... | collective-permute-start | bytes 786440 | tf_op jit(solution)/shard_map/ppermute | solution.py:718
  24.8 4.4 %collective-permute-start.4 = (bf16[8,2048]{1,0:T(8,128)(2,1)S(1)}, bf16[8,2048]{1,0:T(8,128)(2,1)S(1)}, u32[]{:S(2)}, u32[]{:S(2)}) collective-permute-start(bf16[8,2048]{1,0:T(8,128)(2,1)S(1)} %get-tuple-element.71), channel_id=1, source_target_pairs={{3,5},{7,9},{11,13},{15,17},{19,21},{23,25},{27,29},{4,2},{8,6},{1... | collective-permute-start | bytes 98312 | tf_op jit(solution)/shard_map/ppermute | solution.py:738
  25.5 3.8 %collective-permute-start.5 = (bf16[8,2048]{1,0:T(8,128)(2,1)S(1)}, bf16[8,2048]{1,0:T(8,128)(2,1)S(1)}, u32[]{:S(2)}, u32[]{:S(2)}) collective-permute-start(bf16[8,2048]{1,0:T(8,128)(2,1)S(1)} %get-tuple-element.71), channel_id=1, source_target_pairs={{3,6},{7,10},{11,14},{15,18},{19,22},{23,26},{27,30},{4,3},{8,7},{... | collective-permute-start | bytes 98312 | tf_op jit(solution)/shard_map/ppermute | solution.py:738
  44.5 13.4 %copy-start = (bf16[2048,1024]{1,0:T(8,128)(2,1)S(1)}, bf16[2048,1024]{1,0:T(8,128)(2,1)}, u32[]{:S(2)}) copy-start(bf16[2048,1024]{1,0:T(8,128)(2,1)} %refs_2_.13) | copy-start | bytes 12582916
  47.5 5.2 %collective-permute-start.10 = (bf16[2,136,1024]{2,1,0:T(8,128)(2,1)S(1)}, bf16[2,136,1024]{2,1,0:T(8,128)(2,1)S(1)}, u32[]{:S(2)}, u32[]{:S(2)}) collective-permute-start(bf16[2,136,1024]{2,1,0:T(8,128)(2,1)S(1)} %get-tuple-element.103.mine), channel_id=1, source_target_pairs={{0,4},{4,0},{8,12},{12,8},{16,20},{20,16},{24,28},{28,24},{1,5},{5... | collective-permute-start | bytes 1671176 | tf_op jit(solution)/shard_map/ppermute | solution.py:764
  53.4 7.5 %collective-permute-start.11 = (bf16[136,512]{1,0:T(8,128)(2,1)S(1)}, bf16[136,512]{1,0:T(8,128)(2,1)S(1)}, u32[]{:S(2)}, u32[]{:S(2)}) collective-permute-start(bf16[136,512]{1,0:T(8,128)(2,1)S(1)} %get-tuple-element.104), channel_id=1, source_target_pairs={{0,8},{4,12},{8,16},{12,20},{16,24},{20,28},{24,0},{28,4},{1,9},{5... | collective-permute-start | bytes 417800 | tf_op jit(solution)/shard_map/ppermute | solution.py:774
  54.9 8.4 %collective-permute-start.12 = (bf16[136,512]{1,0:T(8,128)(2,1)S(1)}, bf16[136,512]{1,0:T(8,128)(2,1)S(1)}, u32[]{:S(2)}, u32[]{:S(2)}) collective-permute-start(bf16[136,512]{1,0:T(8,128)(2,1)S(1)} %get-tuple-element.105), channel_id=1, source_target_pairs={{0,16},{4,20},{8,24},{12,28},{16,0},{20,4},{24,8},{28,12},{1,17},{... | collective-permute-start | bytes 417800 | tf_op jit(solution)/shard_map/ppermute | solution.py:774
  56.1 7.3 %collective-permute-start.13 = (bf16[136,512]{1,0:T(8,128)(2,1)S(1)}, bf16[136,512]{1,0:T(8,128)(2,1)S(1)}, u32[]{:S(2)}, u32[]{:S(2)}) collective-permute-start(bf16[136,512]{1,0:T(8,128)(2,1)S(1)} %get-tuple-element.106), channel_id=1, source_target_pairs={{0,24},{4,28},{8,0},{12,4},{16,8},{20,12},{24,16},{28,20},{1,25},{... | collective-permute-start | bytes 417800 | tf_op jit(solution)/shard_map/ppermute | solution.py:774
  64.1 4.6 %collective-permute-start.14 = (bf16[2,128,512]{2,1,0:T(8,128)(2,1)S(1)}, bf16[2,128,512]{2,1,0:T(8,128)(2,1)S(1)}, u32[]{:S(2)}, u32[]{:S(2)}) collective-permute-start(bf16[2,128,512]{2,1,0:T(8,128)(2,1)S(1)} %entering.1.mine), channel_id=1, source_target_pairs={{0,4},{4,0},{8,12},{12,8},{16,20},{20,16},{24,28},{28,24},{1,5},{5... | collective-permute-start | bytes 786440 | tf_op jit(solution)/shard_map/ppermute | solution.py:779
  65.0 3.7 %copy-start.2 = (bf16[1024,2048]{1,0:T(8,128)(2,1)S(1)}, bf16[1024,2048]{1,0:T(8,128)(2,1)}, u32[]{:S(2)}) copy-start(bf16[1024,2048]{1,0:T(8,128)(2,1)} %w_out.7) | copy-start | bytes 12582916
  65.0 3.7 %copy-start.6 = (f32[1024]{0:T(1024)S(1)}, f32[1024]{0:T(1024)}, u32[]{:S(2)}) copy-start(f32[1024]{0:T(1024)} %param.20) | copy-start | bytes 12292
  70.5 11.9 %collective-permute-start.15 = (bf16[65,16,128]{2,1,0:T(8,128)(2,1)S(1)}, bf16[65,16,128]{2,1,0:T(8,128)(2,1)S(1)}, u32[]{:S(2)}, u32[]{:S(2)}) collective-permute-start(bf16[65,16,128]{2,1,0:T(8,128)(2,1)S(1)} %get-tuple-element.118), channel_id=1, source_target_pairs={{0,1},{1,2},{2,3},{3,0},{4,5},{5,6},{6,7},{7,4},{8,9},{9,10},{10,1... | collective-permute-start | bytes 798728 | tf_op jit(solution)/shard_map/ppermute | solution.py:715
  72.6 15.0 %collective-permute-start.19 = (bf16[65,16,128]{2,1,0:T(8,128)(2,1)S(1)}, bf16[65,16,128]{2,1,0:T(8,128)(2,1)S(1)}, u32[]{:S(2)}, u32[]{:S(2)}) collective-permute-start(bf16[65,16,128]{2,1,0:T(8,128)(2,1)S(1)} %get-tuple-element.126), channel_id=1, source_target_pairs={{0,3},{1,0},{2,1},{3,2},{4,7},{5,4},{6,5},{7,6},{8,11},{9,8},{10,9... | collective-permute-start | bytes 798728 | tf_op jit(solution)/shard_map/ppermute | solution.py:718
  78.5 20.9 %collective-permute-start.17 = (bf16[65,16,128]{2,1,0:T(8,128)(2,1)S(1)}, bf16[65,16,128]{2,1,0:T(8,128)(2,1)S(1)}, u32[]{:S(2)}, u32[]{:S(2)}) collective-permute-start(bf16[65,16,128]{2,1,0:T(8,128)(2,1)S(1)} %get-tuple-element.123), channel_id=1, source_target_pairs={{0,3},{1,0},{2,1},{3,2},{4,7},{5,4},{6,5},{7,6},{8,11},{9,8},{10,9... | collective-permute-start | bytes 798728 | tf_op jit(solution)/shard_map/ppermute | solution.py:718
  82.3 17.1 %collective-permute-start.18 = (bf16[65,16,128]{2,1,0:T(8,128)(2,1)S(1)}, bf16[65,16,128]{2,1,0:T(8,128)(2,1)S(1)}, u32[]{:S(2)}, u32[]{:S(2)}) collective-permute-start(bf16[65,16,128]{2,1,0:T(8,128)(2,1)S(1)} %get-tuple-element.124), channel_id=1, source_target_pairs={{0,1},{1,2},{2,3},{3,0},{4,5},{5,6},{6,7},{7,4},{8,9},{9,10},{10,1... | collective-permute-start | bytes 798728 | tf_op jit(solution)/shard_map/ppermute | solution.py:715
  82.5 22.5 %collective-permute-start.16 = (bf16[65,16,128]{2,1,0:T(8,128)(2,1)S(1)}, bf16[65,16,128]{2,1,0:T(8,128)(2,1)S(1)}, u32[]{:S(2)}, u32[]{:S(2)}) collective-permute-start(bf16[65,16,128]{2,1,0:T(8,128)(2,1)S(1)} %plus.2), channel_id=1, source_target_pairs={{0,1},{1,2},{2,3},{3,0},{4,5},{5,6},{6,7},{7,4},{8,9},{9,10},{10,1... | collective-permute-start | bytes 798728 | tf_op jit(solution)/shard_map/ppermute | solution.py:715
  87.7 22.0 %collective-permute-start.20 = (bf16[65,16,128]{2,1,0:T(8,128)(2,1)S(1)}, bf16[65,16,128]{2,1,0:T(8,128)(2,1)S(1)}, u32[]{:S(2)}, u32[]{:S(2)}) collective-permute-start(bf16[65,16,128]{2,1,0:T(8,128)(2,1)S(1)} %plus.3), channel_id=1, source_target_pairs={{0,3},{1,0},{2,1},{3,2},{4,7},{5,4},{6,5},{7,6},{8,11},{9,8},{10,9... | collective-permute-start | bytes 798728 | tf_op jit(solution)/shard_map/ppermute | solution.py:718
where the time goes:
time: 111 us
  starting transfers between devices  41.5 us (37%)
  Pallas kernels  35.7 us (32%)
  waiting for transfers between devices  32 us (29%)
    ppermute x6, starting transfers between devices, down(): return lax.ppermute(v, 'row', ring_pairs(ring, -1))  20.4 us
    ppermute x6, waiting for transfers between devices, down(): return lax.ppermute(v, 'row', ring_pairs(ring, -1))  17 us
    pallas_call x4, Pallas kernels, block_states(): pl.pallas_call(body, in_specs=[smem()] + [vmem()] * (count + around + 5),...  12.6 us
    ppermute x6, starting transfers between devices, up(): return lax.ppermute(v, 'row', ring_pairs(ring, 1))  9.68 us
    ppermute x6, waiting for transfers between devices, up(): return lax.ppermute(v, 'row', ring_pairs(ring, 1))  9.59 us
    pallas_call x4, Pallas kernels, finish(): pl.pallas_call(body, grid=(1,), in_specs=specs, out_specs=[vmem()] * len(...  7.13 us
    ppermute x3, starting transfers between devices, layer(): received.append((k, lax.ppermute(sends[k - 1], 'frame', pairs)))  4.49 us
    ppermute x3, waiting for transfers between devices, layer(): received.append((k, lax.ppermute(sends[k - 1], 'frame', pairs)))  3.81 us
  transfers between devices with their start and end apart: 21, of which 12 were waited for; matrix products, arithmetic and copies ran while one was open for 0% of the time, Pallas kernels for 22%

commit v1 on v0

--- a/solution.py
+++ b/solution.py
@@ -11,6 +11,7 @@
 HEAD_DIM = 64
 LANES = 128
 LOGS = 8
+FIRST = 1
 SPLIT = 20_000_000_000
 LOG2E = 1.0 / math.log(2.0)
 F32 = jnp.float32
@@ -263,70 +264,153 @@
     return [dot(packed, spread[d]) for d in range(2)]
 
 
-def combine(where, xfs, xbs, ends, b_ts, fades, lasts, taps, spread, heads):
-    ring = len(xfs)
-    rows, channels = xfs[0].shape
-    size = b_ts[0].shape[1]
+def early_sums(where, early, late, ring, blocks, bounded, taps, spread, heads):
+    rows, channels = blocks[0][0].shape
+    size = blocks[0][4].shape[1]
     pad = 8
     reach = taps.shape[1] - 1
+    count = len(early)
+    needed = [[blocks[k][i] for k in early] for i in (0, 1, 2, 4, 8)]
 
     def body(where, *refs):
-        xf, xb, ends, b_t, fades, lasts = (refs[i * ring : (i + 1) * ring] for i in range(6))
-        taps, spread, pack, fixed, qs, carried, b_all = refs[6 * ring :]
-        at, logs, between = frame_logs(where, lasts, ring)
-        forward = lax.broadcasted_iota(jnp.int32, logs[0].shape, 1) < heads
-        for k in range(ring):
-            later = jnp.where(forward, between(at[k], ring), between(-1, at[k]))
-            qs[k * rows : (k + 1) * rows, :] = two_parts(fades[k][...] * jnp.exp2(later), 2 * heads)
-            for d in range(2):
-                b_all[d, :, k * rows : (k + 1) * rows] = b_t[k][d]
-            first, final = at[k] == 0, at[k] == ring - 1
-            below, above = ends[(k - 1) % ring], ends[(k + 1) % ring]
+        xf, xb, ends, b_t, fades = (dict(zip(early, refs[i * count : (i + 1) * count])) for i in range(5))
+        taps, spread, fixed, added, qs = refs[5 * count :]
+        row = lax.broadcasted_iota(jnp.int32, (rows, LANES), 0)
+        forward = lax.broadcasted_iota(jnp.int32, (rows, LANES), 1) < heads
+        fixed[...] = jnp.zeros_like(fixed)
+        for i, k in enumerate(early):
+            at = lax.rem(where[0] + k, ring)
+            below, above = (k - 1) % ring, (k + 1) % ring
+            fade = fades[k][...]
+            if below == late:
+                fade = jnp.where(forward & (row < pad), 0.0, fade)
+            if above == late:
+                fade = jnp.where(jnp.logical_not(forward) & (row >= rows - pad), 0.0, fade)
+            qs[i * rows : (i + 1) * rows, :] = two_parts(fade, 2 * heads)
             for n in range(0, channels, 256):
                 cols = slice(n, n + 256)
                 own = ends[k][: 2 * pad, cols].astype(F32)
-                before = jnp.where(first, ends[1][2 * pad : 3 * pad, cols], below[pad : 2 * pad, cols])
-                after = jnp.where(final, ends[1][3 * pad :, cols], above[:pad, cols])
-                window = jnp.concatenate([before.astype(F32), own[:pad]], axis=0)
-                fixed[k, :pad, cols] = conv_of(
-                    window[pad - reach :], taps[0, :, cols], False, pad
-                ).astype(BF16)
-                window = jnp.concatenate([own[pad:], after.astype(F32)], axis=0)
-                fixed[k, pad:, cols] = conv_of(
-                    window[: pad + reach], taps[1, :, cols], True, pad
-                ).astype(BF16)
+                if below != late:
+                    outer = ends[bounded][2 * pad : 3 * pad, cols]
+                    before = jnp.where(at == 0, outer, ends[below][pad : 2 * pad, cols]).astype(F32)
+                    window = jnp.concatenate([before, own[:pad]], axis=0)
+                    fixed[k, :pad, cols] = conv_of(
+                        window[pad - reach :], taps[0, :, cols], False, pad
+                    ).astype(BF16)
+                if above != late:
+                    outer = ends[bounded][3 * pad :, cols]
+                    after = jnp.where(at == ring - 1, outer, ends[above][:pad, cols]).astype(F32)
+                    window = jnp.concatenate([own[pad:], after], axis=0)
+                    fixed[k, pad:, cols] = conv_of(
+                        window[: pad + reach], taps[1, :, cols], True, pad
+                    ).astype(BF16)
+        for d in range(2):
+            for n in range(0, channels, 256):
+                cols = slice(n, n + 256)
+                scale = dot(qs[...], spread[d, :, cols])
+                for i, k in enumerate(early):
+                    x = patched((xf, xb)[d][k], fixed, k, cols, pad, d)
+                    part = slice(i * rows, (i + 1) * rows)
+                    added[i, d, :, cols] = dot(b_t[k][d], (scale[part] * x.astype(F32)).astype(BF16))
+
+    return pl.pallas_call(
+        body,
+        in_specs=[smem()] + [vmem()] * (5 * count + 2),
+        out_specs=[vmem()] * 2,
+        out_shape=[
+            jax.ShapeDtypeStruct((ring, 2 * pad, channels), BF16),
+            jax.ShapeDtypeStruct((count, 2, size, channels), F32),
+        ],
+        scratch_shapes=[pltpu.VMEM((count * rows, LANES), BF16)],
+        compiler_params=mib(16),
+        cost_estimate=pl.CostEstimate(flops=1_000_000_000, bytes_accessed=4 << 20, transcendentals=0),
+        name="early_sums",
+    )(where, *[v for group in needed for v in group], taps, spread)
+
+
+def combine(where, early, late, ring, blocks, bounded, lasts, fixed, added, taps, spread, heads):
+    rows, channels = blocks[0][0].shape
+    size = blocks[0][4].shape[1]
+    pad = 8
+    reach = taps.shape[1] - 1
+    below, above = (late - 1) % ring, (late + 1) % ring
+    sides = {k: i for i, k in enumerate(dict.fromkeys((late, below, above, bounded)))}
+    count = len(sides)
+    needed = [blocks[k][i] for i in (2, 4, 8) for k in sides]
+
+    def body(where, *refs):
+        ends, b_t, fades = (
+            {k: refs[i * count + j] for k, j in sides.items()} for i in range(3)
+        )
+        refs = refs[3 * count :]
+        xf, xb, early_fixed, added = refs[:4]
+        lasts = refs[4 : 4 + ring]
+        taps, spread, pack, fixed, carried = refs[4 + ring :]
+        at, logs, between = frame_logs(where, lasts, ring)
+        forward = lax.broadcasted_iota(jnp.int32, logs[0].shape, 1) < heads
+        later = [jnp.where(forward, between(p, ring), between(-1, p)) for p in at]
+        fixed[...] = early_fixed[...]
+
+        def mend(k, d):
+            first, final = at[k] == 0, at[k] == ring - 1
+            for n in range(0, channels, 256):
+                cols = slice(n, n + 256)
+                own = ends[k][: 2 * pad, cols].astype(F32)
+                if d == 0:
+                    outer = ends[bounded][2 * pad : 3 * pad, cols]
+                    next_to = ends[(k - 1) % ring][pad : 2 * pad, cols]
+                    before = jnp.where(first, outer, next_to).astype(F32)
+                    window = jnp.concatenate([before, own[:pad]], axis=0)[pad - reach :]
+                    fixed[k, :pad, cols] = conv_of(window, taps[0, :, cols], False, pad).astype(BF16)
+                else:
+                    outer = ends[bounded][3 * pad :, cols]
+                    next_to = ends[(k + 1) % ring][:pad, cols]
+                    after = jnp.where(final, outer, next_to).astype(F32)
+                    window = jnp.concatenate([own[pad:], after], axis=0)[: pad + reach]
+                    fixed[k, pad:, cols] = conv_of(window, taps[1, :, cols], True, pad).astype(BF16)
+
+        for k, d in ((late, 0), (late, 1), (above, 0), (below, 1)):
+            mend(k, d)
+        q = two_parts(fades[late][...] * jnp.exp2(later[late]), 2 * heads)
+        q_above = two_parts(fades[above][:pad, :] * jnp.exp2(later[above]), 2 * heads)
+        q_below = two_parts(fades[below][rows - pad :, :] * jnp.exp2(later[below]), 2 * heads)
+        weights = spread_rows([later[k] for k in early], heads, spread)
         total = sum(logs[1:], logs[0])
         l1 = total.astype(BF16).astype(F32)
         l2 = (total - l1).astype(BF16).astype(F32)
         three = jnp.concatenate([l1, l2, total - l1 - l2, jnp.zeros((LOGS - 3, LANES), F32)], axis=0)
+        carried[...] = jnp.zeros_like(carried)
         for d in range(2):
             pack[d, size:, :] = dot(three.astype(BF16), spread[d]).astype(BF16)
+            side = above if d == 0 else below
+            place = slice(rows, rows + pad) if d == 0 else slice(2 * rows - pad, 2 * rows)
+            b_all = jnp.concatenate([b_t[late][d], b_t[side][d]], axis=1)
             for n in range(0, channels, 256):
                 cols = slice(n, n + 256)
-                scale = dot(qs[...], spread[d, :, cols])
-                for k in range(ring):
-                    x = patched((xf, xb)[d][k], fixed, k, cols, pad, d)
-                    part = slice(k * rows, (k + 1) * rows)
-                    carried[part, :] = (scale[part] * x.astype(F32)).astype(BF16)
-                pack[d, :size, cols] = dot(b_all[d], carried[...]).astype(BF16)
-
-    return pl.pallas_call(
-        body,
-        in_specs=[smem()] + [vmem()] * (6 * ring + 2),
+                x = patched((xf, xb)[d], fixed, late, cols, pad, d)
+                scale = dot(q, spread[d, :, cols])
+                carried[d, :rows, :] = (scale * x.astype(F32)).astype(BF16)
+                scale = dot(q_above if d == 0 else q_below, spread[d, :, cols])
+                x = fixed[side, :pad, cols] if d == 0 else fixed[side, pad:, cols]
+                carried[d, place, :] = (scale * x.astype(F32)).astype(BF16)
+                state = dot(b_all, carried[d])
+                for i in range(len(early)):
+                    state += weights[d][i : i + 1, cols] * added[i, d, :, cols]
+                pack[d, :size, cols] = state.astype(BF16)
+
+    return pl.pallas_call(
+        body,
+        in_specs=[smem()] + [vmem()] * (3 * count + 6 + ring),
         out_specs=[vmem()] * 2,
         out_shape=[
             jax.ShapeDtypeStruct((2, size + LOGS, channels), BF16),
             jax.ShapeDtypeStruct((ring, 2 * pad, channels), BF16),
         ],
-        scratch_shapes=[
-            pltpu.VMEM((ring * rows, LANES), BF16),
-            pltpu.VMEM((ring * rows, 256), BF16),
-            pltpu.VMEM((2, size, ring * rows), BF16),
-        ],
+        scratch_shapes=[pltpu.VMEM((2, 2 * rows, 256), BF16)],
         compiler_params=mib(16),
-        cost_estimate=pl.CostEstimate(flops=2_000_000_000, bytes_accessed=4 << 20, transcendentals=0),
+        cost_estimate=pl.CostEstimate(flops=500_000_000, bytes_accessed=4 << 20, transcendentals=0),
         name="combine",
-    )(where, *xfs, *xbs, *ends, *b_ts, *fades, *lasts, taps, spread)
+    )(where, *needed, blocks[late][0], blocks[late][1], fixed, added, *lasts, taps, spread)
 
 
 def patched(x, fixed, k, cols, pad, d):
@@ -646,41 +730,39 @@
     )(value, got)
 
 
-def normalize(value, square, halves, channels):
+def normalize(part, into, value, square, got, channels):
     rows, width = value.shape
     half = rows // 2
     across = width // LANES
     count = half // SUB * across
-    each = [len(h) for h in halves]
+    held = [] if into is None else [into]
 
     def body(value, square, *refs):
-        ins, out = refs[:-1], refs[-1]
-        lane = lax.broadcasted_iota(jnp.int32, (1, rows), 1)
-        groups = (ins[: each[0]], ins[each[0] :])
+        ins, out = refs[: len(got)], refs[-1]
         sums = square[0:1, :]
-        for i, group in enumerate(groups):
-            for ref in group:
-                got = squares_of(ref[count])
-                sums = sums + jnp.where((lane >= half) == (i == 1), got, 0.0)
+        for ref in ins:
+            sums = sums + squares_of(ref[count])
         scale = lax.rsqrt(sums / channels + 1e-05)
-        scale = jnp.broadcast_to(scale, (LANES, rows)).T
-        for i in range(rows // SUB):
-            group = groups[i * SUB // half]
+        scale = jnp.broadcast_to(scale, (LANES, rows)).T[part * half : (part + 1) * half]
+        for i in range(half // SUB):
             for j in range(across):
                 at = (slice(i * SUB, (i + 1) * SUB), slice(j * LANES, (j + 1) * LANES))
                 total = value[at]
-                for ref in group:
-                    total = total + ref[i % (half // SUB) * across + j].astype(F32)
+                for ref in ins:
+                    total = total + ref[i * across + j].astype(F32)
                 out[at] = (total * scale[at[0], :]).astype(BF16)
 
-    return pl.pallas_call(
-        body,
-        in_specs=[vmem()] * (2 + sum(each)),
-        out_specs=vmem(),
+    block = pl.BlockSpec((half, width), lambda n: (part, 0))
+    return pl.pallas_call(
+        body,
+        grid=(1,),
+        in_specs=[block] + [vmem()] * (1 + len(got)) + [pl.BlockSpec(memory_space=pl.ANY)] * len(held),
+        out_specs=block,
         out_shape=jax.ShapeDtypeStruct(value.shape, BF16),
+        input_output_aliases={2 + len(got): 0} if held else {},
         compiler_params=mib(8),
         name="normalize",
-    )(value, square, *halves[0], *halves[1])
+    )(value, square, *got, *held)
 
 
 def ring_pairs(count, step):
@@ -742,10 +824,11 @@
     gain = norm_gain.reshape(1, -1)
 
     blocks = {}
+    bounded = order[-2]
     for k in order:
         blocks[k] = block_states(
             pieces[k],
-            bounds if k == 1 else [],
+            bounds if k == bounded else [],
             where,
             w_value,
             w_state_proj,
@@ -754,10 +837,13 @@
             small_rows,
             heads,
         )
-    xfs, xbs, ends, bcs, b_ts, cums, cum_ts, reached, fading, lasts = (
+    xfs, xbs, _, bcs, b_ts, cums, cum_ts, reached, fading, lasts = (
         [blocks[k][i] for k in range(ring)] for i in range(len(blocks[0]))
     )
-    pack, fixed = combine(where, xfs, xbs, ends, b_ts, fading, lasts, conv_taps, spread, heads)
+    early, late = order[:-1], order[-1]
+    shared = (early, late, ring, blocks, bounded)
+    fixed, added = early_sums(where, *shared, conv_taps, spread, heads)
+    pack, fixed = combine(where, *shared, lasts, fixed, added, conv_taps, spread, heads)
 
     if span == 2:
         swap = [(i, i ^ 1) for i in range(frames)]
@@ -814,7 +900,9 @@
         down_b = down(below_b if down_b is None else plus(below_b, down_b))
     value, square = block(0)
     halves = [[v for v in pair if v is not None] for pair in ((up_a, down_a), (up_b, down_b))]
-    return normalize(value, square, halves, channels * ring).reshape(tokens.shape)
+    mixed = normalize(FIRST, None, value, square, halves[FIRST], channels * ring)
+    mixed = normalize(1 - FIRST, mixed, value, square, halves[1 - FIRST], channels * ring)
+    return mixed.reshape(tokens.shape)
 
 
 def solution(mesh):

time: 111 us -> 116 us (1.045)
  starting transfers between devices: 41.5 us -> 48.2 us
  waiting for transfers between devices: 32 us -> 29 us
  Pallas kernels: 35.7 us -> 37.4 us
    ppermute x6, starting transfers between devices: 9.68 us -> 14.6 us  [up(): return lax.ppermute(v, 'row', ring_pairs(ring, 1))]
    ppermute x6, waiting for transfers between devices: 9.59 us -> 5.33 us  [up(): return lax.ppermute(v, 'row', ring_pairs(ring, 1))]
    ppermute x3, starting transfers between devices: 4.49 us -> 7.17 us  [layer(): received.append((k, lax.ppermute(sends[k - 1], 'frame', pairs)))]
    ppermute x6, waiting for transfers between devices: 17 us -> 18.5 us  [down(): return lax.ppermute(v, 'row', ring_pairs(ring, -1))]
    pallas_call x2 -> x4, Pallas kernels: 4.01 us -> 5.46 us  [the longest x1 2.06 us: combine(): pl.pallas_call(body, in_specs=[smem()] + [vmem()] * (3 * count + 6 + ring...]
  transfers between devices with their start and end apart: 21 -> 21, of which waited for: 12 -> 8; matrix products, arithmetic and copies ran while one was open for 0% -> 0% of each run, Pallas kernels for 22% -> 24%
where the time goes in v1:
time: 116 us
  starting transfers between devices  48.2 us (42%)
  Pallas kernels  37.4 us (32%)
  waiting for transfers between devices  29 us (25%)
    ppermute x6, starting transfers between devices, down(): return lax.ppermute(v, 'row', ring_pairs(ring, -1))  19.7 us
    ppermute x6, waiting for transfers between devices, down(): return lax.ppermute(v, 'row', ring_pairs(ring, -1))  18.5 us
    ppermute x6, starting transfers between devices, up(): return lax.ppermute(v, 'row', ring_pairs(ring, 1))  14.6 us
    pallas_call x4, Pallas kernels, block_states(): pl.pallas_call(body, in_specs=[smem()] + [vmem()] * (count + around + 5),...  12.8 us
    ppermute x3, starting transfers between devices, layer(): received.append((k, lax.ppermute(sends[k - 1], 'frame', pairs)))  7.17 us
    pallas_call x4, Pallas kernels, finish(): pl.pallas_call(body, grid=(1,), in_specs=specs, out_specs=[vmem()] * len(...  7.13 us
    ppermute x6, waiting for transfers between devices, up(): return lax.ppermute(v, 'row', ring_pairs(ring, 1))  5.33 us
    pallas_call x4, Pallas kernels, inside(): pl.pallas_call(body, in_specs=[vmem()] * 7, out_specs=vmem(), out_shape=j...  3.61 us
  transfers between devices with their start and end apart: 21, of which 8 were waited for; matrix products, arithmetic and copies ran while one was open for 0% of the time, Pallas kernels for 24%

profile of v1, /device:TPU:0, one launch (start us, length us, event | category | flops | bytes accessed | tf_op | source)
XLA Modules:
  0.0 116.0 jit_solution(17184186525933387059)
XLA Ops:
  0.0 0.1 pad_add_fusion.where
  0.1 1.0 copy-done.10
  1.1 0.0 copy-start.3
  1.1 0.0 copy-start.4
  1.2 0.0 copy-start.5
  1.2 0.6 split.1
  1.8 3.1 %collective-permute-start = (bf16[64,2048]{1,0:T(8,128)(2,1)S(1)}, bf16[64,2048]{1,0:T(8,128)(2,1)S(1)}, u32[]{:S(2)}, u32[]{:S(2)}) collective-permute-start(bf16[64,2048]{1,0:T(8,128)(2,1)S(1)} %get-tuple-element.68.refs_0_), channel_id=1, source_target_pairs={{0,1},{1,2},{2,3},{3,0},{4,5},{5,6},{6,7},{7,4},{8,9},{9,10},{10,1... | collective-permute-start | bytes 786440 | tf_op jit(solution)/shard_map/ppermute | solution.py:797
  4.9 2.1 %collective-permute-start.2 = (bf16[64,2048]{1,0:T(8,128)(2,1)S(1)}, bf16[64,2048]{1,0:T(8,128)(2,1)S(1)}, u32[]{:S(2)}, u32[]{:S(2)}) collective-permute-start(bf16[64,2048]{1,0:T(8,128)(2,1)S(1)} %get-tuple-element.69.refs_1_), channel_id=1, source_target_pairs={{0,3},{1,0},{2,1},{3,2},{4,7},{5,4},{6,5},{7,6},{8,11},{9,8},{10,9... | collective-permute-start | bytes 786440 | tf_op jit(solution)/shard_map/ppermute | solution.py:800
  7.0 0.0 collective-permute-start.9
  7.0 1.3 %collective-permute-start.5 = (bf16[8,2048]{1,0:T(8,128)(2,1)S(1)}, bf16[8,2048]{1,0:T(8,128)(2,1)S(1)}, u32[]{:S(2)}, u32[]{:S(2)}) collective-permute-start(bf16[8,2048]{1,0:T(8,128)(2,1)S(1)} %get-tuple-element.74), channel_id=1, source_target_pairs={{3,7},{7,11},{11,15},{15,19},{19,23},{23,27},{27,31},{4,0},{8,4},{... | collective-permute-start | bytes 98312 | tf_op jit(solution)/shard_map/ppermute | solution.py:820
  8.2 3.9 %collective-permute-start.4 = (bf16[64,2048]{1,0:T(8,128)(2,1)S(1)}, bf16[64,2048]{1,0:T(8,128)(2,1)S(1)}, u32[]{:S(2)}, u32[]{:S(2)}) collective-permute-start(bf16[64,2048]{1,0:T(8,128)(2,1)S(1)} %get-tuple-element.68.refs_0_), channel_id=1, source_target_pairs={{0,3},{1,0},{2,1},{3,2},{4,7},{5,4},{6,5},{7,6},{8,11},{9,8},{10,9... | collective-permute-start | bytes 786440 | tf_op jit(solution)/shard_map/ppermute | solution.py:800
  12.1 0.2 prepare.1
  12.3 0.7 collective-permute-start.6
  13.0 3.1 %block_states.4 = (bf16[128,1024]{1,0:T(8,128)(2,1)S(1)}, bf16[128,1024]{1,0:T(8,128)(2,1)S(1)}, bf16[16,1024]{1,0:T(8,128)(2,1)S(1)}, bf16[128,512]{1,0:T(8,128...) custom-call(s32[3]{0:T(128)S(1)} %pad_add_fusion.where, ...), custom_call_target="tpu_custom_call" | custom-call | flops 1308622848 | bytes 6815744 | tf_op jit(solution)/shard_map/block_states/pallas_call | solution.py:227
  16.1 0.7 collective-permute-start.7
  16.8 0.7 collective-permute-start.8
  17.5 2.3 %collective-permute-done.2.refs_1_ = bf16[64,2048]{1,0:T(8,128)(2,1)S(1)} collective-permute-done((bf16[64,2048]{1,0:T(8,128)(2,1)S(1)}, bf16[64,2048]{1,0:T(8,128)(2,1)S(1)}, u32[]{:S(2)}, u32[]{:S(2)}) %collective-permute-start.2) | collective-permute-done | bytes 262176 | tf_op jit(solution)/shard_map/ppermute | solution.py:800
  19.8 11.0 %collective-permute-start.1 = (bf16[64,2048]{1,0:T(8,128)(2,1)S(1)}, bf16[64,2048]{1,0:T(8,128)(2,1)S(1)}, u32[]{:S(2)}, u32[]{:S(2)}) collective-permute-start(bf16[64,2048]{1,0:T(8,128)(2,1)S(1)} %collective-permute-done.refs_0_), channel_id=1, source_target_pairs={{0,1},{1,2},{2,3},{3,0},{4,5},{5,6},{6,7},{7,4},{8,9},{9,10},{10,1... | collective-permute-start | bytes 786440 | tf_op jit(solution)/shard_map/ppermute | solution.py:797
  30.8 6.4 %collective-permute-start.3 = (bf16[64,2048]{1,0:T(8,128)(2,1)S(1)}, bf16[64,2048]{1,0:T(8,128)(2,1)S(1)}, u32[]{:S(2)}, u32[]{:S(2)}) collective-permute-start(bf16[64,2048]{1,0:T(8,128)(2,1)S(1)} %collective-permute-done.2.refs_1_), channel_id=1, source_target_pairs={{0,3},{1,0},{2,1},{3,2},{4,7},{5,4},{6,5},{7,6},{8,11},{9,8},{10,9... | collective-permute-start | bytes 786440 | tf_op jit(solution)/shard_map/ppermute | solution.py:800
  37.2 3.1 %block_states.7 = (bf16[128,1024]{1,0:T(8,128)(2,1)S(1)}, bf16[128,1024]{1,0:T(8,128)(2,1)S(1)}, bf16[16,1024]{1,0:T(8,128)(2,1)S(1)}, bf16[128,512]{1,0:T(8,128...) custom-call(s32[3]{0:T(128)S(1)} %pad_add_fusion.where, ...), custom_call_target="tpu_custom_call" | custom-call | flops 1308622848 | bytes 6815744 | tf_op jit(solution)/shard_map/block_states/pallas_call | solution.py:227
  40.3 3.5 %block_states.6 = (bf16[128,1024]{1,0:T(8,128)(2,1)S(1)}, bf16[128,1024]{1,0:T(8,128)(2,1)S(1)}, bf16[32,1024]{1,0:T(8,128)(2,1)S(1)}, bf16[128,512]{1,0:T(8,128...) custom-call(s32[3]{0:T(128)S(1)} %pad_add_fusion.where, ...), custom_call_target="tpu_custom_call" | custom-call | flops 1472200704 | bytes 6815744 | tf_op jit(solution)/shard_map/block_states/pallas_call | solution.py:227
  43.8 1.7 %early_sums.1 = (bf16[4,16,1024]{2,1,0:T(8,128)(2,1)S(1)}, f32[3,2,128,1024]{3,2,1,0:T(8,128)S(1)}) custom-call(s32[3]{0:T(128)S(1)} %pad_add_fusion.where, bf16[128,1024]{1,0:T(8,128)(2,1)S(1)} %get-tuple-element.71.refs_0_.xf, bf16[128,1024]{1,0:T(8,128)(2,1)S(1)} %get-tuple-element.85.refs_1_.refs_3_.xf, ...), custom_call_target="tpu_custom_call" | custom-call | flops 1000000000 | bytes 4194304 | tf_op jit(solution)/shard_map/early_sums/pallas_call | solution.py:316
  45.6 3.1 %block_states.5 = (bf16[128,1024]{1,0:T(8,128)(2,1)S(1)}, bf16[128,1024]{1,0:T(8,128)(2,1)S(1)}, bf16[16,1024]{1,0:T(8,128)(2,1)S(1)}, bf16[128,512]{1,0:T(8,128...) custom-call(s32[3]{0:T(128)S(1)} %pad_add_fusion.where, ...), custom_call_target="tpu_custom_call" | custom-call | flops 1308622848 | bytes 6815744 | tf_op jit(solution)/shard_map/block_states/pallas_call | solution.py:227
  48.7 0.0 copy-start.1
  48.7 2.1 %combine.1 = (bf16[2,136,1024]{2,1,0:T(8,128)(2,1)S(1)}, bf16[4,16,1024]{2,1,0:T(8,128)(2,1)S(1)}) custom-call(s32[3]{0:T(128)S(1)} %pad_add_fusion.where, bf16[16,1024]{1,0:T(8,128)(2,1)S(1)} %get-tuple-element.73.refs_0_, bf16[32,1024]{1,0:T(8,128)(2,1)S(1)} %get-tuple-element.75.refs_8_.refs_1_, bf16[16,1024]{1,0:T(8,128)(2,1)S(1)} %get-tuple-element.76.refs_7_.refs_2_, ...), custom_call_target="tpu_custom_call" | custom-call | flops 500000000 | bytes 4194304 | tf_op jit(solution)/shard_map/combine/pallas_call | solution.py:401
  50.7 3.4 %collective-permute-start.10 = (bf16[2,136,1024]{2,1,0:T(8,128)(2,1)S(1)}, bf16[2,136,1024]{2,1,0:T(8,128)(2,1)S(1)}, u32[]{:S(2)}, u32[]{:S(2)}) collective-permute-start(bf16[2,136,1024]{2,1,0:T(8,128)(2,1)S(1)} %get-tuple-element.107.mine), channel_id=1, source_target_pairs={{0,4},{4,0},{8,12},{12,8},{16,20},{20,16},{24,28},{28,24},{1,5},{5... | collective-permute-start | bytes 1671176 | tf_op jit(solution)/shard_map/ppermute | solution.py:850
  54.1 1.6 %collective-permute-done.10.theirs = bf16[2,136,1024]{2,1,0:T(8,128)(2,1)S(1)} collective-permute-done((bf16[2,136,1024]{2,1,0:T(8,128)(2,1)S(1)}, bf16[2,136,1024]{2,1,0:T(8,128)(2,1)S(1)}, u32[]{:S(2)}, u32[]{:S(2)}) %collective-permute-start.10) | collective-permute-done | bytes 557088 | tf_op jit(solution)/shard_map/ppermute | solution.py:850
  55.7 0.7 messages.1
  56.4 4.2 %collective-permute-start.11 = (bf16[136,512]{1,0:T(8,128)(2,1)S(1)}, bf16[136,512]{1,0:T(8,128)(2,1)S(1)}, u32[]{:S(2)}, u32[]{:S(2)}) collective-permute-start(bf16[136,512]{1,0:T(8,128)(2,1)S(1)} %get-tuple-element.108), channel_id=1, source_target_pairs={{0,8},{4,12},{8,16},{12,20},{16,24},{20,28},{24,0},{28,4},{1,9},{5... | collective-permute-start | bytes 417800 | tf_op jit(solution)/shard_map/ppermute | solution.py:860
  60.6 0.2 collective-permute-start.12
  60.7 2.8 %collective-permute-start.13 = (bf16[136,512]{1,0:T(8,128)(2,1)S(1)}, bf16[136,512]{1,0:T(8,128)(2,1)S(1)}, u32[]{:S(2)}, u32[]{:S(2)}) collective-permute-start(bf16[136,512]{1,0:T(8,128)(2,1)S(1)} %get-tuple-element.110), channel_id=1, source_target_pairs={{0,24},{4,28},{8,0},{12,4},{16,8},{20,12},{24,16},{28,20},{1,25},{... | collective-permute-start | bytes 417800 | tf_op jit(solution)/shard_map/ppermute | solution.py:860
  63.6 0.8 gates.5.gate
  64.4 0.8 gates.7.gate
  65.3 1.7 %collective-permute-done.12.refs_1_ = bf16[136,512]{1,0:T(8,128)(2,1)S(1)} collective-permute-done((bf16[136,512]{1,0:T(8,128)(2,1)S(1)}, bf16[136,512]{1,0:T(8,128)(2,1)S(1)}, u32[]{:S(2)}, u32[]{:S(2)}) %collective-permute-start.12) | collective-permute-done | bytes 139296 | tf_op jit(solution)/shard_map/ppermute | solution.py:860
  66.9 1.9 %collective-permute-done.13.refs_2_ = bf16[136,512]{1,0:T(8,128)(2,1)S(1)} collective-permute-done((bf16[136,512]{1,0:T(8,128)(2,1)S(1)}, bf16[136,512]{1,0:T(8,128)(2,1)S(1)}, u32[]{:S(2)}, u32[]{:S(2)}) %collective-permute-start.13) | collective-permute-done | bytes 139296 | tf_op jit(solution)/shard_map/ppermute | solution.py:860
  68.8 0.7 entering.1.mine
  69.5 0.1 collective-permute-start.14
  69.6 0.8 gates.6.gate
  70.5 0.0 copy-start.2
  70.5 0.0 copy-start.6
  70.5 2.7 %starts.1 = (f32[4,2,128,1024]{3,2,1,0:T(8,128)S(1)}, f32[2,8,1024]{2,1,0:T(8,128)S(1)}) custom-call(s32[3]{0:T(128)S(1)} %pad_add_fusion.where, bf16[128,1024]{1,0:T(8,128)(2,1)S(1)} %get-tuple-element.71.refs_0_.xf, bf16[128,1024]{1,0:T(8,128)(2,1)S(1)} %get-tuple-element.86.refs_2_.refs_1_.xf, bf16[128,1024]{1,0:T(8,128)(2,1)S(1)} %get-tuple-element.83.refs_9_.refs_2_.xf, ...), custom_call_target="tpu_custom_call" | custom-call | flops 1200000000 | bytes 8388608 | tf_op jit(solution)/shard_map/starts/pallas_call | solution.py:470
  73.2 0.9 inside.6.y
  74.2 1.8 %finish.6 = (bf16[65,16,128]{2,1,0:T(8,128)(2,1)S(1)}, bf16[65,16,128]{2,1,0:T(8,128)(2,1)S(1)}) custom-call(s32[3]{0:T(128)S(1)} %pad_add_fusion.where, f32[128,1024]{1,0:T(8,128)S(1)} %inside.6.y, bf16[128,512]{1,0:T(8,128)(2,1)S(1)} %get-tuple-element.118.bc, bf16[128,128]{1,0:T(8,128)(2,1)S(1)} %get-tuple-element.121.reached, ...), custom_call_target="tpu_custom_call" | custom-call | flops 536870912 | bytes 4194304 | tf_op jit(solution)/shard_map/finish/pallas_call | solution.py:699
  75.9 0.1 collective-permute-start.15
  76.0 3.8 %collective-permute-start.19 = (bf16[65,16,128]{2,1,0:T(8,128)(2,1)S(1)}, bf16[65,16,128]{2,1,0:T(8,128)(2,1)S(1)}, u32[]{:S(2)}, u32[]{:S(2)}) collective-permute-start(bf16[65,16,128]{2,1,0:T(8,128)(2,1)S(1)} %get-tuple-element.130), channel_id=1, source_target_pairs={{0,3},{1,0},{2,1},{3,2},{4,7},{5,4},{6,5},{7,6},{8,11},{9,8},{10,9... | collective-permute-start | bytes 798728 | tf_op jit(solution)/shard_map/ppermute | solution.py:800
  79.8 0.9 inside.5.y
  80.7 0.9 inside.7.y
  81.6 1.8 %finish.5 = (bf16[65,16,128]{2,1,0:T(8,128)(2,1)S(1)}, bf16[65,16,128]{2,1,0:T(8,128)(2,1)S(1)}) custom-call(s32[3]{0:T(128)S(1)} %pad_add_fusion.where, f32[128,1024]{1,0:T(8,128)S(1)} %inside.5.y, bf16[128,512]{1,0:T(8,128)(2,1)S(1)} %get-tuple-element.113.bc, bf16[128,128]{1,0:T(8,128)(2,1)S(1)} %get-tuple-element.116.reached, ...), custom_call_target="tpu_custom_call" | custom-call | flops 536870912 | bytes 4194304 | tf_op jit(solution)/shard_map/finish/pallas_call | solution.py:699
  83.4 0.1 collective-permute-start.18
  83.5 1.8 %finish.7 = (bf16[65,16,128]{2,1,0:T(8,128)(2,1)S(1)}, bf16[65,16,128]{2,1,0:T(8,128)(2,1)S(1)}) custom-call(s32[3]{0:T(128)S(1)} %pad_add_fusion.where, f32[128,1024]{1,0:T(8,128)S(1)} %inside.7.y, bf16[128,512]{1,0:T(8,128)(2,1)S(1)} %get-tuple-element.123.bc, bf16[128,128]{1,0:T(8,128)(2,1)S(1)} %get-tuple-element.126.reached, ...), custom_call_target="tpu_custom_call" | custom-call | flops 536870912 | bytes 4194304 | tf_op jit(solution)/shard_map/finish/pallas_call | solution.py:699
  85.3 6.1 %collective-permute-done.19.got = bf16[65,16,128]{2,1,0:T(8,128)(2,1)S(1)} collective-permute-done((bf16[65,16,128]{2,1,0:T(8,128)(2,1)S(1)}, bf16[65,16,128]{2,1,0:T(8,128)(2,1)S(1)}, u32[]{:S(2)}, u32[]{:S(2)}) %collective-permute-start.19) | collective-permute-done | bytes 266272 | tf_op jit(solution)/shard_map/ppermute | solution.py:800
  91.4 0.1 plus.3
  91.4 1.5 %collective-permute-start.20 = (bf16[65,16,128]{2,1,0:T(8,128)(2,1)S(1)}, bf16[65,16,128]{2,1,0:T(8,128)(2,1)S(1)}, u32[]{:S(2)}, u32[]{:S(2)}) collective-permute-start(bf16[65,16,128]{2,1,0:T(8,128)(2,1)S(1)} %plus.3), channel_id=1, source_target_pairs={{0,3},{1,0},{2,1},{3,2},{4,7},{5,4},{6,5},{7,6},{8,11},{9,8},{10,9... | collective-permute-start | bytes 798728 | tf_op jit(solution)/shard_map/ppermute | solution.py:800
  92.9 2.0 %collective-permute-start.17 = (bf16[65,16,128]{2,1,0:T(8,128)(2,1)S(1)}, bf16[65,16,128]{2,1,0:T(8,128)(2,1)S(1)}, u32[]{:S(2)}, u32[]{:S(2)}) collective-permute-start(bf16[65,16,128]{2,1,0:T(8,128)(2,1)S(1)} %get-tuple-element.127), channel_id=1, source_target_pairs={{0,3},{1,0},{2,1},{3,2},{4,7},{5,4},{6,5},{7,6},{8,11},{9,8},{10,9... | collective-permute-start | bytes 798728 | tf_op jit(solution)/shard_map/ppermute | solution.py:800
  95.0 0.1 plus.2
  95.0 0.3 collective-permute-start.16
  95.4 0.8 gates.4.gate
  96.2 0.9 inside.4.y
  97.1 1.8 %finish.4 = (f32[128,2048]{1,0:T(8,128)S(1)}, f32[16,128]{1,0:T(8,128)S(1)}) custom-call(s32[3]{0:T(128)S(1)} %pad_add_fusion.where, f32[128,1024]{1,0:T(8,128)S(1)} %inside.4.y, bf16[128,512]{1,0:T(8,128)(2,1)S(1)} %get-tuple-element.100.bc, bf16[128,128]{1,0:T(8,128)(2,1)S(1)} %get-tuple-element.104.reached, f32[128,1024]{1,0:T(8,128)S(1)} %gates.4.gate, ...), custom_call_target="tpu_custom_call" | custom-call | flops 536870912 | bytes 4194304 | tf_op jit(solution)/shard_map/finish/pallas_call | solution.py:699
  98.9 4.9 %collective-permute-done.20.refs_1_ = bf16[65,16,128]{2,1,0:T(8,128)(2,1)S(1)} collective-permute-done((bf16[65,16,128]{2,1,0:T(8,128)(2,1)S(1)}, bf16[65,16,128]{2,1,0:T(8,128)(2,1)S(1)}, u32[]{:S(2)}, u32[]{:S(2)}) %collective-permute-start.20) | collective-permute-done | bytes 266272 | tf_op jit(solution)/shard_map/ppermute | solution.py:800
  103.8 0.9 normalize.2.refs_2_
  104.7 5.2 %collective-permute-done.17.refs_1_ = bf16[65,16,128]{2,1,0:T(8,128)(2,1)S(1)} collective-permute-done((bf16[65,16,128]{2,1,0:T(8,128)(2,1)S(1)}, bf16[65,16,128]{2,1,0:T(8,128)(2,1)S(1)}, u32[]{:S(2)}, u32[]{:S(2)}) %collective-permute-start.17) | collective-permute-done | bytes 266272 | tf_op jit(solution)/shard_map/ppermute | solution.py:800
  109.9 5.3 %collective-permute-done.16.refs_0_ = bf16[65,16,128]{2,1,0:T(8,128)(2,1)S(1)} collective-permute-done((bf16[65,16,128]{2,1,0:T(8,128)(2,1)S(1)}, bf16[65,16,128]{2,1,0:T(8,128)(2,1)S(1)}, u32[]{:S(2)}, u32[]{:S(2)}) %collective-permute-start.16) | collective-permute-done | bytes 266272 | tf_op jit(solution)/shard_map/ppermute | solution.py:797
  115.2 0.8 normalize.3
  (28 shorter events, 0.1 us)
Async XLA Ops:
  0.1 1.0 copy-start.10
  1.1 11.0 %copy-start.7 = (f32[2,16]{1,0:T(2,128)S(1)}, f32[2,16]{1,0:T(2,128)}, u32[]{:S(2)}) copy-start(f32[2,16]{1,0:T(2,128)} %bias.1) | copy-start | bytes 388
  1.1 11.0 %copy-start.8 = (f32[2,16]{1,0:T(2,128)S(1)}, f32[2,16]{1,0:T(2,128)}, u32[]{:S(2)}) copy-start(f32[2,16]{1,0:T(2,128)} %rate.1) | copy-start | bytes 388
  1.1 11.0 %copy-start.9 = (f32[2,16]{1,0:T(2,128)S(1)}, f32[2,16]{1,0:T(2,128)}, u32[]{:S(2)}) copy-start(f32[2,16]{1,0:T(2,128)} %skip.1) | copy-start | bytes 388
  1.1 11.9 %copy-start = (bf16[2048,1024]{1,0:T(8,128)(2,1)S(1)}, bf16[2048,1024]{1,0:T(8,128)(2,1)}, u32[]{:S(2)}) copy-start(bf16[2048,1024]{1,0:T(8,128)(2,1)} %refs_2_.9) | copy-start | bytes 12582916
  1.1 11.9 %copy-start.3 = (bf16[2048,512]{1,0:T(8,128)(2,1)S(1)}, bf16[2048,512]{1,0:T(8,128)(2,1)}, u32[]{:S(2)}) copy-start(bf16[2048,512]{1,0:T(8,128)(2,1)} %refs_3_.5) | copy-start | bytes 6291460
  1.1 11.9 %copy-start.4 = (bf16[2,2048,16]{1,2,0:T(8,128)(2,1)S(1)}, bf16[2,2048,16]{1,2,0:T(8,128)(2,1)}, u32[]{:S(2)}) copy-start(bf16[2,2048,16]{1,2,0:T(8,128)(2,1)} %param.15) | copy-start | bytes 393220
  1.2 11.9 %copy-start.5 = (f32[2,4,1024]{2,1,0:T(4,128)S(1)}, f32[2,4,1024]{2,1,0:T(4,128)}, u32[]{:S(2)}) copy-start(f32[2,4,1024]{2,1,0:T(4,128)} %refs_17_.1) | copy-start | bytes 98308
  1.8 15.0 %collective-permute-start = (bf16[64,2048]{1,0:T(8,128)(2,1)S(1)}, bf16[64,2048]{1,0:T(8,128)(2,1)S(1)}, u32[]{:S(2)}, u32[]{:S(2)}) collective-permute-start(bf16[64,2048]{1,0:T(8,128)(2,1)S(1)} %get-tuple-element.68.refs_0_), channel_id=1, source_target_pairs={{0,1},{1,2},{2,3},{3,0},{4,5},{5,6},{6,7},{7,4},{8,9},{9,10},{10,1... | collective-permute-start | bytes 786440 | tf_op jit(solution)/shard_map/ppermute | solution.py:797
  4.9 14.9 %collective-permute-start.2 = (bf16[64,2048]{1,0:T(8,128)(2,1)S(1)}, bf16[64,2048]{1,0:T(8,128)(2,1)S(1)}, u32[]{:S(2)}, u32[]{:S(2)}) collective-permute-start(bf16[64,2048]{1,0:T(8,128)(2,1)S(1)} %get-tuple-element.69.refs_1_), channel_id=1, source_target_pairs={{0,3},{1,0},{2,1},{3,2},{4,7},{5,4},{6,5},{7,6},{8,11},{9,8},{10,9... | collective-permute-start | bytes 786440 | tf_op jit(solution)/shard_map/ppermute | solution.py:800
  7.0 23.8 %collective-permute-start.9 = (bf16[64,2048]{1,0:T(8,128)(2,1)S(1)}, bf16[64,2048]{1,0:T(8,128)(2,1)S(1)}, u32[]{:S(2)}, u32[]{:S(2)}) collective-permute-start(bf16[64,2048]{1,0:T(8,128)(2,1)S(1)} %get-tuple-element.69.refs_1_), channel_id=1, source_target_pairs={{0,1},{1,2},{2,3},{3,0},{4,5},{5,6},{6,7},{7,4},{8,9},{9,10},{10,1... | collective-permute-start | bytes 786440 | tf_op jit(solution)/shard_map/ppermute | solution.py:797
  7.0 5.4 %collective-permute-start.5 = (bf16[8,2048]{1,0:T(8,128)(2,1)S(1)}, bf16[8,2048]{1,0:T(8,128)(2,1)S(1)}, u32[]{:S(2)}, u32[]{:S(2)}) collective-permute-start(bf16[8,2048]{1,0:T(8,128)(2,1)S(1)} %get-tuple-element.74), channel_id=1, source_target_pairs={{3,7},{7,11},{11,15},{15,19},{19,23},{23,27},{27,31},{4,0},{8,4},{... | collective-permute-start | bytes 98312 | tf_op jit(solution)/shard_map/ppermute | solution.py:820
  8.2 32.1 %collective-permute-start.4 = (bf16[64,2048]{1,0:T(8,128)(2,1)S(1)}, bf16[64,2048]{1,0:T(8,128)(2,1)S(1)}, u32[]{:S(2)}, u32[]{:S(2)}) collective-permute-start(bf16[64,2048]{1,0:T(8,128)(2,1)S(1)} %get-tuple-element.68.refs_0_), channel_id=1, source_target_pairs={{0,3},{1,0},{2,1},{3,2},{4,7},{5,4},{6,5},{7,6},{8,11},{9,8},{10,9... | collective-permute-start | bytes 786440 | tf_op jit(solution)/shard_map/ppermute | solution.py:800
  12.3 3.8 %collective-permute-start.6 = (bf16[8,2048]{1,0:T(8,128)(2,1)S(1)}, bf16[8,2048]{1,0:T(8,128)(2,1)S(1)}, u32[]{:S(2)}, u32[]{:S(2)}) collective-permute-start(bf16[8,2048]{1,0:T(8,128)(2,1)S(1)} %get-tuple-element.74), channel_id=1, source_target_pairs={{3,4},{7,8},{11,12},{15,16},{19,20},{23,24},{27,28},{4,1},{8,5},{1... | collective-permute-start | bytes 98312 | tf_op jit(solution)/shard_map/ppermute | solution.py:820
  16.1 24.2 %collective-permute-start.7 = (bf16[8,2048]{1,0:T(8,128)(2,1)S(1)}, bf16[8,2048]{1,0:T(8,128)(2,1)S(1)}, u32[]{:S(2)}, u32[]{:S(2)}) collective-permute-start(bf16[8,2048]{1,0:T(8,128)(2,1)S(1)} %get-tuple-element.74), channel_id=1, source_target_pairs={{3,5},{7,9},{11,13},{15,17},{19,21},{23,25},{27,29},{4,2},{8,6},{1... | collective-permute-start | bytes 98312 | tf_op jit(solution)/shard_map/ppermute | solution.py:820
  16.8 23.5 %collective-permute-start.8 = (bf16[8,2048]{1,0:T(8,128)(2,1)S(1)}, bf16[8,2048]{1,0:T(8,128)(2,1)S(1)}, u32[]{:S(2)}, u32[]{:S(2)}) collective-permute-start(bf16[8,2048]{1,0:T(8,128)(2,1)S(1)} %get-tuple-element.74), channel_id=1, source_target_pairs={{3,6},{7,10},{11,14},{15,18},{19,22},{23,26},{27,30},{4,3},{8,7},{... | collective-permute-start | bytes 98312 | tf_op jit(solution)/shard_map/ppermute | solution.py:820
  19.8 25.8 %collective-permute-start.1 = (bf16[64,2048]{1,0:T(8,128)(2,1)S(1)}, bf16[64,2048]{1,0:T(8,128)(2,1)S(1)}, u32[]{:S(2)}, u32[]{:S(2)}) collective-permute-start(bf16[64,2048]{1,0:T(8,128)(2,1)S(1)} %collective-permute-done.refs_0_), channel_id=1, source_target_pairs={{0,1},{1,2},{2,3},{3,0},{4,5},{5,6},{6,7},{7,4},{8,9},{9,10},{10,1... | collective-permute-start | bytes 786440 | tf_op jit(solution)/shard_map/ppermute | solution.py:797
  30.8 14.8 %collective-permute-start.3 = (bf16[64,2048]{1,0:T(8,128)(2,1)S(1)}, bf16[64,2048]{1,0:T(8,128)(2,1)S(1)}, u32[]{:S(2)}, u32[]{:S(2)}) collective-permute-start(bf16[64,2048]{1,0:T(8,128)(2,1)S(1)} %collective-permute-done.2.refs_1_), channel_id=1, source_target_pairs={{0,3},{1,0},{2,1},{3,2},{4,7},{5,4},{6,5},{7,6},{8,11},{9,8},{10,9... | collective-permute-start | bytes 786440 | tf_op jit(solution)/shard_map/ppermute | solution.py:800
  48.7 14.9 %copy-start.1 = (bf16[2048,1024]{1,0:T(8,128)(2,1)S(1)}, bf16[2048,1024]{1,0:T(8,128)(2,1)}, u32[]{:S(2)}) copy-start(bf16[2048,1024]{1,0:T(8,128)(2,1)} %refs_2_.13) | copy-start | bytes 12582916
  50.7 4.9 %collective-permute-start.10 = (bf16[2,136,1024]{2,1,0:T(8,128)(2,1)S(1)}, bf16[2,136,1024]{2,1,0:T(8,128)(2,1)S(1)}, u32[]{:S(2)}, u32[]{:S(2)}) collective-permute-start(bf16[2,136,1024]{2,1,0:T(8,128)(2,1)S(1)} %get-tuple-element.107.mine), channel_id=1, source_target_pairs={{0,4},{4,0},{8,12},{12,8},{16,20},{20,16},{24,28},{28,24},{1,5},{5... | collective-permute-start | bytes 1671176 | tf_op jit(solution)/shard_map/ppermute | solution.py:850
  56.4 8.9 %collective-permute-start.11 = (bf16[136,512]{1,0:T(8,128)(2,1)S(1)}, bf16[136,512]{1,0:T(8,128)(2,1)S(1)}, u32[]{:S(2)}, u32[]{:S(2)}) collective-permute-start(bf16[136,512]{1,0:T(8,128)(2,1)S(1)} %get-tuple-element.108), channel_id=1, source_target_pairs={{0,8},{4,12},{8,16},{12,20},{16,24},{20,28},{24,0},{28,4},{1,9},{5... | collective-permute-start | bytes 417800 | tf_op jit(solution)/shard_map/ppermute | solution.py:860
  60.6 6.4 %collective-permute-start.12 = (bf16[136,512]{1,0:T(8,128)(2,1)S(1)}, bf16[136,512]{1,0:T(8,128)(2,1)S(1)}, u32[]{:S(2)}, u32[]{:S(2)}) collective-permute-start(bf16[136,512]{1,0:T(8,128)(2,1)S(1)} %get-tuple-element.109), channel_id=1, source_target_pairs={{0,16},{4,20},{8,24},{12,28},{16,0},{20,4},{24,8},{28,12},{1,17},{... | collective-permute-start | bytes 417800 | tf_op jit(solution)/shard_map/ppermute | solution.py:860
  60.7 8.1 %collective-permute-start.13 = (bf16[136,512]{1,0:T(8,128)(2,1)S(1)}, bf16[136,512]{1,0:T(8,128)(2,1)S(1)}, u32[]{:S(2)}, u32[]{:S(2)}) collective-permute-start(bf16[136,512]{1,0:T(8,128)(2,1)S(1)} %get-tuple-element.110), channel_id=1, source_target_pairs={{0,24},{4,28},{8,0},{12,4},{16,8},{20,12},{24,16},{28,20},{1,25},{... | collective-permute-start | bytes 417800 | tf_op jit(solution)/shard_map/ppermute | solution.py:860
  69.5 4.6 %collective-permute-start.14 = (bf16[2,128,512]{2,1,0:T(8,128)(2,1)S(1)}, bf16[2,128,512]{2,1,0:T(8,128)(2,1)S(1)}, u32[]{:S(2)}, u32[]{:S(2)}) collective-permute-start(bf16[2,128,512]{2,1,0:T(8,128)(2,1)S(1)} %entering.1.mine), channel_id=1, source_target_pairs={{0,4},{4,0},{8,12},{12,8},{16,20},{20,16},{24,28},{28,24},{1,5},{5... | collective-permute-start | bytes 786440 | tf_op jit(solution)/shard_map/ppermute | solution.py:865
  70.5 3.7 %copy-start.2 = (bf16[1024,2048]{1,0:T(8,128)(2,1)S(1)}, bf16[1024,2048]{1,0:T(8,128)(2,1)}, u32[]{:S(2)}) copy-start(bf16[1024,2048]{1,0:T(8,128)(2,1)} %w_out.7) | copy-start | bytes 12582916
  70.5 3.7 %copy-start.6 = (f32[1024]{0:T(1024)S(1)}, f32[1024]{0:T(1024)}, u32[]{:S(2)}) copy-start(f32[1024]{0:T(1024)} %param.20) | copy-start | bytes 12292
  75.9 19.0 %collective-permute-start.15 = (bf16[65,16,128]{2,1,0:T(8,128)(2,1)S(1)}, bf16[65,16,128]{2,1,0:T(8,128)(2,1)S(1)}, u32[]{:S(2)}, u32[]{:S(2)}) collective-permute-start(bf16[65,16,128]{2,1,0:T(8,128)(2,1)S(1)} %get-tuple-element.122), channel_id=1, source_target_pairs={{0,1},{1,2},{2,3},{3,0},{4,5},{5,6},{6,7},{7,4},{8,9},{9,10},{10,1... | collective-permute-start | bytes 798728 | tf_op jit(solution)/shard_map/ppermute | solution.py:797
  76.0 15.4 %collective-permute-start.19 = (bf16[65,16,128]{2,1,0:T(8,128)(2,1)S(1)}, bf16[65,16,128]{2,1,0:T(8,128)(2,1)S(1)}, u32[]{:S(2)}, u32[]{:S(2)}) collective-permute-start(bf16[65,16,128]{2,1,0:T(8,128)(2,1)S(1)} %get-tuple-element.130), channel_id=1, source_target_pairs={{0,3},{1,0},{2,1},{3,2},{4,7},{5,4},{6,5},{7,6},{8,11},{9,8},{10,9... | collective-permute-start | bytes 798728 | tf_op jit(solution)/shard_map/ppermute | solution.py:800
  83.4 15.5 %collective-permute-start.18 = (bf16[65,16,128]{2,1,0:T(8,128)(2,1)S(1)}, bf16[65,16,128]{2,1,0:T(8,128)(2,1)S(1)}, u32[]{:S(2)}, u32[]{:S(2)}) collective-permute-start(bf16[65,16,128]{2,1,0:T(8,128)(2,1)S(1)} %get-tuple-element.128), channel_id=1, source_target_pairs={{0,1},{1,2},{2,3},{3,0},{4,5},{5,6},{6,7},{7,4},{8,9},{9,10},{10,1... | collective-permute-start | bytes 798728 | tf_op jit(solution)/shard_map/ppermute | solution.py:797
  91.4 12.4 %collective-permute-start.20 = (bf16[65,16,128]{2,1,0:T(8,128)(2,1)S(1)}, bf16[65,16,128]{2,1,0:T(8,128)(2,1)S(1)}, u32[]{:S(2)}, u32[]{:S(2)}) collective-permute-start(bf16[65,16,128]{2,1,0:T(8,128)(2,1)S(1)} %plus.3), channel_id=1, source_target_pairs={{0,3},{1,0},{2,1},{3,2},{4,7},{5,4},{6,5},{7,6},{8,11},{9,8},{10,9... | collective-permute-start | bytes 798728 | tf_op jit(solution)/shard_map/ppermute | solution.py:800
  92.9 16.9 %collective-permute-start.17 = (bf16[65,16,128]{2,1,0:T(8,128)(2,1)S(1)}, bf16[65,16,128]{2,1,0:T(8,128)(2,1)S(1)}, u32[]{:S(2)}, u32[]{:S(2)}) collective-permute-start(bf16[65,16,128]{2,1,0:T(8,128)(2,1)S(1)} %get-tuple-element.127), channel_id=1, source_target_pairs={{0,3},{1,0},{2,1},{3,2},{4,7},{5,4},{6,5},{7,6},{8,11},{9,8},{10,9... | collective-permute-start | bytes 798728 | tf_op jit(solution)/shard_map/ppermute | solution.py:800
  95.0 20.2 %collective-permute-start.16 = (bf16[65,16,128]{2,1,0:T(8,128)(2,1)S(1)}, bf16[65,16,128]{2,1,0:T(8,128)(2,1)S(1)}, u32[]{:S(2)}, u32[]{:S(2)}) collective-permute-start(bf16[65,16,128]{2,1,0:T(8,128)(2,1)S(1)} %plus.2), channel_id=1, source_target_pairs={{0,1},{1,2},{2,3},{3,0},{4,5},{5,6},{6,7},{7,4},{8,9},{9,10},{10,1... | collective-permute-start | bytes 798728 | tf_op jit(solution)/shard_map/ppermute | solution.py:797

commit v2 on v1

--- a/solution.py
+++ b/solution.py
@@ -121,7 +121,7 @@
     return silu(total)
 
 
-def block_states(pieces, bounds, where, w_value, w_state, w_step, taps, small_rows, heads):
+def block_states(pieces, bounds, where, w_value, w_state, w_step, taps, small_rows, heads, brief):
     rows, depth = sum(p.shape[0] for p in pieces), pieces[0].shape[1]
     channels, states, steps = w_value.shape[1], w_state.shape[1], w_step.shape[0]
     size = states // 4
@@ -177,8 +177,10 @@
         raw = jnp.concatenate(
             [raw.astype(BF16).astype(F32), jnp.zeros((rows, LANES - steps), F32)], axis=1
         )
-        for n in range(0, states, 256):
-            bc[:, n : n + 256] = dot(stacked[:rows, :], ws[:, n : n + 256]).astype(BF16)
+        wide = 2 * size
+        for n in range(0, states, wide):
+            cols = slice(n, n + (size if brief else wide))
+            bc[:, cols] = dot(stacked[:rows, :], ws[:, cols]).astype(BF16)
         conv(channels - 256)
 
         lane = lax.broadcasted_iota(jnp.int32, (rows, LANES), 1)
@@ -529,29 +531,42 @@
     )(xf, xb, fixed, bc, cum, cum_t, skip)
 
 
-def gates(pieces, w_gate):
+def gates(pieces, w_gate, bc=None, w_state=None):
     rows, depth = sum(p.shape[0] for p in pieces), pieces[0].shape[1]
     channels, count = w_gate.shape[1], len(pieces)
+    more = [] if bc is None else [bc, w_state]
+    size = 0 if bc is None else bc.shape[1] // 4
 
     def body(*refs):
-        wg, gate, block = refs[count:]
+        wg, refs_ = refs[count], refs[count + 1 + len(more) :]
+        gate, block = refs_[0], refs_[-1]
         gather(refs[:count], block)
+        if more:
+            old, ws, new = refs[count + 1], refs[count + 2], refs_[1]
+            for d in range(2):
+                b_cols = slice(2 * d * size, (2 * d + 1) * size)
+                c_cols = slice((2 * d + 1) * size, (2 * d + 2) * size)
+                new[:, b_cols] = old[:, b_cols]
+                new[:, c_cols] = dot(block[...], ws[:, c_cols]).astype(BF16)
         for n in range(0, channels, 256):
             raw = dot(block[...], wg[:, n : n + 256]).astype(BF16)
             gate[:, n : n + 256] = silu(raw.astype(F32))
 
-    return pl.pallas_call(
-        body,
-        in_specs=[vmem()] * (count + 1),
-        out_specs=vmem(),
-        out_shape=jax.ShapeDtypeStruct((rows, channels), F32),
+    shapes = [jax.ShapeDtypeStruct((rows, channels), F32)]
+    if more:
+        shapes.append(jax.ShapeDtypeStruct(bc.shape, BF16))
+    return pl.pallas_call(
+        body,
+        in_specs=[vmem()] * (count + 1 + len(more)),
+        out_specs=[vmem()] * len(shapes),
+        out_shape=shapes,
         scratch_shapes=[pltpu.VMEM((rows, depth), BF16)],
         compiler_params=mib(12),
         cost_estimate=pl.CostEstimate(
             flops=2 * rows * depth * channels, bytes_accessed=2 * depth * channels, transcendentals=0
         ),
         name="gates",
-    )(*pieces, w_gate)
+    )(*pieces, w_gate, *more)
 
 
 def log_rows(rows):
@@ -836,6 +851,7 @@
             conv_taps,
             small_rows,
             heads,
+            k == order[-1],
         )
     xfs, xbs, _, bcs, b_ts, cums, cum_ts, reached, fading, lasts = (
         [blocks[k][i] for k in range(ring)] for i in range(len(blocks[0]))
@@ -865,8 +881,11 @@
     other = lax.ppermute(enter, "frame", swap) if span == 2 else enter
     inner, gate = {}, {}
     for k in order:
+        if k == late:
+            gate[k], bcs[k] = gates(pieces[k], w_gate, bcs[k], w_state_proj)
+        else:
+            (gate[k],) = gates(pieces[k], w_gate)
         inner[k] = inside(k, xfs[k], xbs[k], fixed, bcs[k], cums[k], cum_ts[k], skip, heads)
-        gate[k] = gates(pieces[k], w_gate)
     starts, fades = starts_of(where, xfs, xbs, fixed, b_ts, fading, lasts, spread, heads)
 
     def block(k):

time: 116 us -> 117 us (level)
  no operation moved by 1% of the time
where the time goes in v2:
time: 117 us; the launch traced here: 116 us
  starting transfers between devices  48.2 us (41%)
  Pallas kernels  37.6 us (32%)
  waiting for transfers between devices  29 us (25%)
    ppermute x6, starting transfers between devices, down(): return lax.ppermute(v, 'row', ring_pairs(ring, -1))  19.7 us
    ppermute x6, waiting for transfers between devices, down(): return lax.ppermute(v, 'row', ring_pairs(ring, -1))  18.5 us
    ppermute x6, starting transfers between devices, up(): return lax.ppermute(v, 'row', ring_pairs(ring, 1))  14.6 us
    pallas_call x4, Pallas kernels, block_states(): pl.pallas_call(body, in_specs=[smem()] + [vmem()] * (count + around + 5),...  12.8 us
    ppermute x3, starting transfers between devices, layer(): received.append((k, lax.ppermute(sends[k - 1], 'frame', pairs)))  7.24 us
    pallas_call x4, Pallas kernels, finish(): pl.pallas_call(body, grid=(1,), in_specs=specs, out_specs=[vmem()] * len(...  7.1 us
    ppermute x6, waiting for transfers between devices, up(): return lax.ppermute(v, 'row', ring_pairs(ring, 1))  5.32 us
    pallas_call x4, Pallas kernels, inside(): pl.pallas_call(body, in_specs=[vmem()] * 7, out_specs=vmem(), out_shape=j...  3.62 us
  transfers between devices with their start and end apart: 21, of which 8 were waited for; matrix products, arithmetic and copies ran while one was open for 0% of the time, Pallas kernels for 24%

profile of v2, /device:TPU:0, one launch (start us, length us, event | category | flops | bytes accessed | tf_op | source)
XLA Modules:
  0.0 116.4 jit_solution(9034386404912447126)
XLA Ops:
  0.0 0.1 pad_add_fusion.where
  0.1 1.0 copy-done.10
  1.1 0.0 copy-start.3
  1.1 0.0 copy-start.4
  1.2 0.0 copy-start.5
  1.2 0.6 split.1
  1.8 3.1 %collective-permute-start = (bf16[64,2048]{1,0:T(8,128)(2,1)S(1)}, bf16[64,2048]{1,0:T(8,128)(2,1)S(1)}, u32[]{:S(2)}, u32[]{:S(2)}) collective-permute-start(bf16[64,2048]{1,0:T(8,128)(2,1)S(1)} %get-tuple-element.70.refs_0_), channel_id=1, source_target_pairs={{0,1},{1,2},{2,3},{3,0},{4,5},{5,6},{6,7},{7,4},{8,9},{9,10},{10,1... | collective-permute-start | bytes 786440 | tf_op jit(solution)/shard_map/ppermute | solution.py:812
  4.9 2.1 %collective-permute-start.2 = (bf16[64,2048]{1,0:T(8,128)(2,1)S(1)}, bf16[64,2048]{1,0:T(8,128)(2,1)S(1)}, u32[]{:S(2)}, u32[]{:S(2)}) collective-permute-start(bf16[64,2048]{1,0:T(8,128)(2,1)S(1)} %get-tuple-element.71.refs_1_), channel_id=1, source_target_pairs={{0,3},{1,0},{2,1},{3,2},{4,7},{5,4},{6,5},{7,6},{8,11},{9,8},{10,9... | collective-permute-start | bytes 786440 | tf_op jit(solution)/shard_map/ppermute | solution.py:815
  7.0 0.0 collective-permute-start.9
  7.0 1.3 %collective-permute-start.5 = (bf16[8,2048]{1,0:T(8,128)(2,1)S(1)}, bf16[8,2048]{1,0:T(8,128)(2,1)S(1)}, u32[]{:S(2)}, u32[]{:S(2)}) collective-permute-start(bf16[8,2048]{1,0:T(8,128)(2,1)S(1)} %get-tuple-element.76), channel_id=1, source_target_pairs={{3,7},{7,11},{11,15},{15,19},{19,23},{23,27},{27,31},{4,0},{8,4},{... | collective-permute-start | bytes 98312 | tf_op jit(solution)/shard_map/ppermute | solution.py:835
  8.2 3.9 %collective-permute-start.4 = (bf16[64,2048]{1,0:T(8,128)(2,1)S(1)}, bf16[64,2048]{1,0:T(8,128)(2,1)S(1)}, u32[]{:S(2)}, u32[]{:S(2)}) collective-permute-start(bf16[64,2048]{1,0:T(8,128)(2,1)S(1)} %get-tuple-element.70.refs_0_), channel_id=1, source_target_pairs={{0,3},{1,0},{2,1},{3,2},{4,7},{5,4},{6,5},{7,6},{8,11},{9,8},{10,9... | collective-permute-start | bytes 786440 | tf_op jit(solution)/shard_map/ppermute | solution.py:815
  12.1 0.2 prepare.1
  12.3 0.7 collective-permute-start.6
  13.0 3.1 %block_states.4 = (bf16[128,1024]{1,0:T(8,128)(2,1)S(1)}, bf16[128,1024]{1,0:T(8,128)(2,1)S(1)}, bf16[16,1024]{1,0:T(8,128)(2,1)S(1)}, bf16[128,512]{1,0:T(8,128...) custom-call(s32[3]{0:T(128)S(1)} %pad_add_fusion.where, ...), custom_call_target="tpu_custom_call" | custom-call | flops 1308622848 | bytes 6815744 | tf_op jit(solution)/shard_map/block_states/pallas_call | solution.py:229
  16.1 0.7 collective-permute-start.7
  16.8 0.7 collective-permute-start.8
  17.5 2.3 %collective-permute-done.2.refs_1_ = bf16[64,2048]{1,0:T(8,128)(2,1)S(1)} collective-permute-done((bf16[64,2048]{1,0:T(8,128)(2,1)S(1)}, bf16[64,2048]{1,0:T(8,128)(2,1)S(1)}, u32[]{:S(2)}, u32[]{:S(2)}) %collective-permute-start.2) | collective-permute-done | bytes 262176 | tf_op jit(solution)/shard_map/ppermute | solution.py:815
  19.8 11.0 %collective-permute-start.1 = (bf16[64,2048]{1,0:T(8,128)(2,1)S(1)}, bf16[64,2048]{1,0:T(8,128)(2,1)S(1)}, u32[]{:S(2)}, u32[]{:S(2)}) collective-permute-start(bf16[64,2048]{1,0:T(8,128)(2,1)S(1)} %collective-permute-done.refs_0_), channel_id=1, source_target_pairs={{0,1},{1,2},{2,3},{3,0},{4,5},{5,6},{6,7},{7,4},{8,9},{9,10},{10,1... | collective-permute-start | bytes 786440 | tf_op jit(solution)/shard_map/ppermute | solution.py:812
  30.8 6.4 %collective-permute-start.3 = (bf16[64,2048]{1,0:T(8,128)(2,1)S(1)}, bf16[64,2048]{1,0:T(8,128)(2,1)S(1)}, u32[]{:S(2)}, u32[]{:S(2)}) collective-permute-start(bf16[64,2048]{1,0:T(8,128)(2,1)S(1)} %collective-permute-done.2.refs_1_), channel_id=1, source_target_pairs={{0,3},{1,0},{2,1},{3,2},{4,7},{5,4},{6,5},{7,6},{8,11},{9,8},{10,9... | collective-permute-start | bytes 786440 | tf_op jit(solution)/shard_map/ppermute | solution.py:815
  37.2 3.1 %block_states.7 = (bf16[128,1024]{1,0:T(8,128)(2,1)S(1)}, bf16[128,1024]{1,0:T(8,128)(2,1)S(1)}, bf16[16,1024]{1,0:T(8,128)(2,1)S(1)}, bf16[128,512]{1,0:T(8,128...) custom-call(s32[3]{0:T(128)S(1)} %pad_add_fusion.where, ...), custom_call_target="tpu_custom_call" | custom-call | flops 1308622848 | bytes 6815744 | tf_op jit(solution)/shard_map/block_states/pallas_call | solution.py:229
  40.3 3.5 %block_states.6 = (bf16[128,1024]{1,0:T(8,128)(2,1)S(1)}, bf16[128,1024]{1,0:T(8,128)(2,1)S(1)}, bf16[32,1024]{1,0:T(8,128)(2,1)S(1)}, bf16[128,512]{1,0:T(8,128...) custom-call(s32[3]{0:T(128)S(1)} %pad_add_fusion.where, ...), custom_call_target="tpu_custom_call" | custom-call | flops 1472200704 | bytes 6815744 | tf_op jit(solution)/shard_map/block_states/pallas_call | solution.py:229
  43.8 1.7 %early_sums.1 = (bf16[4,16,1024]{2,1,0:T(8,128)(2,1)S(1)}, f32[3,2,128,1024]{3,2,1,0:T(8,128)S(1)}) custom-call(s32[3]{0:T(128)S(1)} %pad_add_fusion.where, bf16[128,1024]{1,0:T(8,128)(2,1)S(1)} %get-tuple-element.73.refs_0_.xf, bf16[128,1024]{1,0:T(8,128)(2,1)S(1)} %get-tuple-element.87.refs_1_.refs_3_.xf, ...), custom_call_target="tpu_custom_call" | custom-call | flops 1000000000 | bytes 4194304 | tf_op jit(solution)/shard_map/early_sums/pallas_call | solution.py:318
  45.5 3.2 %block_states.5 = (bf16[128,1024]{1,0:T(8,128)(2,1)S(1)}, bf16[128,1024]{1,0:T(8,128)(2,1)S(1)}, bf16[16,1024]{1,0:T(8,128)(2,1)S(1)}, bf16[128,512]{1,0:T(8,128...) custom-call(s32[3]{0:T(128)S(1)} %pad_add_fusion.where, ...), custom_call_target="tpu_custom_call" | custom-call | flops 1308622848 | bytes 6815744 | tf_op jit(solution)/shard_map/block_states/pallas_call | solution.py:229
  48.7 0.0 copy-start.1
  48.7 2.1 %combine.1 = (bf16[2,136,1024]{2,1,0:T(8,128)(2,1)S(1)}, bf16[4,16,1024]{2,1,0:T(8,128)(2,1)S(1)}) custom-call(s32[3]{0:T(128)S(1)} %pad_add_fusion.where, bf16[16,1024]{1,0:T(8,128)(2,1)S(1)} %get-tuple-element.75.refs_0_, bf16[32,1024]{1,0:T(8,128)(2,1)S(1)} %get-tuple-element.77.refs_8_.refs_1_, bf16[16,1024]{1,0:T(8,128)(2,1)S(1)} %get-tuple-element.78.refs_7_.refs_2_, ...), custom_call_target="tpu_custom_call" | custom-call | flops 500000000 | bytes 4194304 | tf_op jit(solution)/shard_map/combine/pallas_call | solution.py:403
  50.8 3.4 %collective-permute-start.10 = (bf16[2,136,1024]{2,1,0:T(8,128)(2,1)S(1)}, bf16[2,136,1024]{2,1,0:T(8,128)(2,1)S(1)}, u32[]{:S(2)}, u32[]{:S(2)}) collective-permute-start(bf16[2,136,1024]{2,1,0:T(8,128)(2,1)S(1)} %get-tuple-element.109.mine), channel_id=1, source_target_pairs={{0,4},{4,0},{8,12},{12,8},{16,20},{20,16},{24,28},{28,24},{1,5},{5... | collective-permute-start | bytes 1671176 | tf_op jit(solution)/shard_map/ppermute | solution.py:866
  54.1 1.6 %collective-permute-done.10.theirs = bf16[2,136,1024]{2,1,0:T(8,128)(2,1)S(1)} collective-permute-done((bf16[2,136,1024]{2,1,0:T(8,128)(2,1)S(1)}, bf16[2,136,1024]{2,1,0:T(8,128)(2,1)S(1)}, u32[]{:S(2)}, u32[]{:S(2)}) %collective-permute-start.10) | collective-permute-done | bytes 557088 | tf_op jit(solution)/shard_map/ppermute | solution.py:866
  55.7 0.7 messages.1
  56.4 4.2 %collective-permute-start.11 = (bf16[136,512]{1,0:T(8,128)(2,1)S(1)}, bf16[136,512]{1,0:T(8,128)(2,1)S(1)}, u32[]{:S(2)}, u32[]{:S(2)}) collective-permute-start(bf16[136,512]{1,0:T(8,128)(2,1)S(1)} %get-tuple-element.110), channel_id=1, source_target_pairs={{0,8},{4,12},{8,16},{12,20},{16,24},{20,28},{24,0},{28,4},{1,9},{5... | collective-permute-start | bytes 417800 | tf_op jit(solution)/shard_map/ppermute | solution.py:876
  60.6 0.2 collective-permute-start.12
  60.8 2.8 %collective-permute-start.13 = (bf16[136,512]{1,0:T(8,128)(2,1)S(1)}, bf16[136,512]{1,0:T(8,128)(2,1)S(1)}, u32[]{:S(2)}, u32[]{:S(2)}) collective-permute-start(bf16[136,512]{1,0:T(8,128)(2,1)S(1)} %get-tuple-element.112), channel_id=1, source_target_pairs={{0,24},{4,28},{8,0},{12,4},{16,8},{20,12},{24,16},{28,20},{1,25},{... | collective-permute-start | bytes 417800 | tf_op jit(solution)/shard_map/ppermute | solution.py:876
  63.7 0.8 gates.5.gate
  64.5 0.8 gates.7.gate
  65.3 1.7 %collective-permute-done.12.refs_1_ = bf16[136,512]{1,0:T(8,128)(2,1)S(1)} collective-permute-done((bf16[136,512]{1,0:T(8,128)(2,1)S(1)}, bf16[136,512]{1,0:T(8,128)(2,1)S(1)}, u32[]{:S(2)}, u32[]{:S(2)}) %collective-permute-start.12) | collective-permute-done | bytes 139296 | tf_op jit(solution)/shard_map/ppermute | solution.py:876
  67.0 1.9 %collective-permute-done.13.refs_2_ = bf16[136,512]{1,0:T(8,128)(2,1)S(1)} collective-permute-done((bf16[136,512]{1,0:T(8,128)(2,1)S(1)}, bf16[136,512]{1,0:T(8,128)(2,1)S(1)}, u32[]{:S(2)}, u32[]{:S(2)}) %collective-permute-start.13) | collective-permute-done | bytes 139296 | tf_op jit(solution)/shard_map/ppermute | solution.py:876
  68.9 0.7 entering.1.mine
  69.6 0.1 collective-permute-start.14
  69.7 1.1 gates.6
  70.8 0.0 copy-start.2
  70.8 0.0 copy-start.6
  70.8 2.7 %starts.1 = (f32[4,2,128,1024]{3,2,1,0:T(8,128)S(1)}, f32[2,8,1024]{2,1,0:T(8,128)S(1)}) custom-call(s32[3]{0:T(128)S(1)} %pad_add_fusion.where, bf16[128,1024]{1,0:T(8,128)(2,1)S(1)} %get-tuple-element.73.refs_0_.xf, bf16[128,1024]{1,0:T(8,128)(2,1)S(1)} %get-tuple-element.88.refs_2_.refs_1_.xf, bf16[128,1024]{1,0:T(8,128)(2,1)S(1)} %get-tuple-element.85.refs_9_.refs_2_.xf, ...), custom_call_target="tpu_custom_call" | custom-call | flops 1200000000 | bytes 8388608 | tf_op jit(solution)/shard_map/starts/pallas_call | solution.py:472
  73.6 0.9 inside.6.y
  74.5 1.8 %finish.6 = (bf16[65,16,128]{2,1,0:T(8,128)(2,1)S(1)}, bf16[65,16,128]{2,1,0:T(8,128)(2,1)S(1)}) custom-call(s32[3]{0:T(128)S(1)} %pad_add_fusion.where, f32[128,1024]{1,0:T(8,128)S(1)} %inside.6.y, bf16[128,512]{1,0:T(8,128)(2,1)S(1)} %get-tuple-element.121.bc, bf16[128,128]{1,0:T(8,128)(2,1)S(1)} %get-tuple-element.124.reached, ...), custom_call_target="tpu_custom_call" | custom-call | flops 536870912 | bytes 4194304 | tf_op jit(solution)/shard_map/finish/pallas_call | solution.py:714
  76.3 0.1 collective-permute-start.15
  76.3 3.8 %collective-permute-start.19 = (bf16[65,16,128]{2,1,0:T(8,128)(2,1)S(1)}, bf16[65,16,128]{2,1,0:T(8,128)(2,1)S(1)}, u32[]{:S(2)}, u32[]{:S(2)}) collective-permute-start(bf16[65,16,128]{2,1,0:T(8,128)(2,1)S(1)} %get-tuple-element.134), channel_id=1, source_target_pairs={{0,3},{1,0},{2,1},{3,2},{4,7},{5,4},{6,5},{7,6},{8,11},{9,8},{10,9... | collective-permute-start | bytes 798728 | tf_op jit(solution)/shard_map/ppermute | solution.py:815
  80.2 0.9 inside.5.y
  81.1 0.9 inside.7.y
  82.0 1.8 %finish.5 = (bf16[65,16,128]{2,1,0:T(8,128)(2,1)S(1)}, bf16[65,16,128]{2,1,0:T(8,128)(2,1)S(1)}) custom-call(s32[3]{0:T(128)S(1)} %pad_add_fusion.where, f32[128,1024]{1,0:T(8,128)S(1)} %inside.5.y, bf16[128,512]{1,0:T(8,128)(2,1)S(1)} %get-tuple-element.115.bc, bf16[128,128]{1,0:T(8,128)(2,1)S(1)} %get-tuple-element.118.reached, ...), custom_call_target="tpu_custom_call" | custom-call | flops 536870912 | bytes 4194304 | tf_op jit(solution)/shard_map/finish/pallas_call | solution.py:714
  83.8 0.1 collective-permute-start.18
  83.8 1.8 %finish.7 = (bf16[65,16,128]{2,1,0:T(8,128)(2,1)S(1)}, bf16[65,16,128]{2,1,0:T(8,128)(2,1)S(1)}) custom-call(s32[3]{0:T(128)S(1)} %pad_add_fusion.where, f32[128,1024]{1,0:T(8,128)S(1)} %inside.7.y, bf16[128,512]{1,0:T(8,128)(2,1)S(1)} %get-tuple-element.127.bc, bf16[128,128]{1,0:T(8,128)(2,1)S(1)} %get-tuple-element.130.reached, ...), custom_call_target="tpu_custom_call" | custom-call | flops 536870912 | bytes 4194304 | tf_op jit(solution)/shard_map/finish/pallas_call | solution.py:714
  85.6 6.1 %collective-permute-done.19.got = bf16[65,16,128]{2,1,0:T(8,128)(2,1)S(1)} collective-permute-done((bf16[65,16,128]{2,1,0:T(8,128)(2,1)S(1)}, bf16[65,16,128]{2,1,0:T(8,128)(2,1)S(1)}, u32[]{:S(2)}, u32[]{:S(2)}) %collective-permute-start.19) | collective-permute-done | bytes 266272 | tf_op jit(solution)/shard_map/ppermute | solution.py:815
  91.7 0.1 plus.3
  91.8 1.5 %collective-permute-start.20 = (bf16[65,16,128]{2,1,0:T(8,128)(2,1)S(1)}, bf16[65,16,128]{2,1,0:T(8,128)(2,1)S(1)}, u32[]{:S(2)}, u32[]{:S(2)}) collective-permute-start(bf16[65,16,128]{2,1,0:T(8,128)(2,1)S(1)} %plus.3), channel_id=1, source_target_pairs={{0,3},{1,0},{2,1},{3,2},{4,7},{5,4},{6,5},{7,6},{8,11},{9,8},{10,9... | collective-permute-start | bytes 798728 | tf_op jit(solution)/shard_map/ppermute | solution.py:815
  93.3 2.0 %collective-permute-start.17 = (bf16[65,16,128]{2,1,0:T(8,128)(2,1)S(1)}, bf16[65,16,128]{2,1,0:T(8,128)(2,1)S(1)}, u32[]{:S(2)}, u32[]{:S(2)}) collective-permute-start(bf16[65,16,128]{2,1,0:T(8,128)(2,1)S(1)} %get-tuple-element.131), channel_id=1, source_target_pairs={{0,3},{1,0},{2,1},{3,2},{4,7},{5,4},{6,5},{7,6},{8,11},{9,8},{10,9... | collective-permute-start | bytes 798728 | tf_op jit(solution)/shard_map/ppermute | solution.py:815
  95.3 0.1 plus.2
  95.4 0.3 collective-permute-start.16
  95.7 0.8 gates.4.gate
  96.5 0.9 inside.4.y
  97.4 1.8 %finish.4 = (f32[128,2048]{1,0:T(8,128)S(1)}, f32[16,128]{1,0:T(8,128)S(1)}) custom-call(s32[3]{0:T(128)S(1)} %pad_add_fusion.where, f32[128,1024]{1,0:T(8,128)S(1)} %inside.4.y, bf16[128,512]{1,0:T(8,128)(2,1)S(1)} %get-tuple-element.102.bc, bf16[128,128]{1,0:T(8,128)(2,1)S(1)} %get-tuple-element.106.reached, f32[128,1024]{1,0:T(8,128)S(1)} %gates.4.gate, ...), custom_call_target="tpu_custom_call" | custom-call | flops 536870912 | bytes 4194304 | tf_op jit(solution)/shard_map/finish/pallas_call | solution.py:714
  99.3 4.9 %collective-permute-done.20.refs_1_ = bf16[65,16,128]{2,1,0:T(8,128)(2,1)S(1)} collective-permute-done((bf16[65,16,128]{2,1,0:T(8,128)(2,1)S(1)}, bf16[65,16,128]{2,1,0:T(8,128)(2,1)S(1)}, u32[]{:S(2)}, u32[]{:S(2)}) %collective-permute-start.20) | collective-permute-done | bytes 266272 | tf_op jit(solution)/shard_map/ppermute | solution.py:815
  104.1 0.9 normalize.2.refs_2_
  105.0 5.2 %collective-permute-done.17.refs_1_ = bf16[65,16,128]{2,1,0:T(8,128)(2,1)S(1)} collective-permute-done((bf16[65,16,128]{2,1,0:T(8,128)(2,1)S(1)}, bf16[65,16,128]{2,1,0:T(8,128)(2,1)S(1)}, u32[]{:S(2)}, u32[]{:S(2)}) %collective-permute-start.17) | collective-permute-done | bytes 266272 | tf_op jit(solution)/shard_map/ppermute | solution.py:815
  110.2 5.3 %collective-permute-done.16.refs_0_ = bf16[65,16,128]{2,1,0:T(8,128)(2,1)S(1)} collective-permute-done((bf16[65,16,128]{2,1,0:T(8,128)(2,1)S(1)}, bf16[65,16,128]{2,1,0:T(8,128)(2,1)S(1)}, u32[]{:S(2)}, u32[]{:S(2)}) %collective-permute-start.16) | collective-permute-done | bytes 266272 | tf_op jit(solution)/shard_map/ppermute | solution.py:812
  115.5 0.8 normalize.3
  (28 shorter events, 0.1 us)
Async XLA Ops:
  0.1 1.0 copy-start.10
  1.1 11.0 %copy-start.7 = (f32[2,16]{1,0:T(2,128)S(1)}, f32[2,16]{1,0:T(2,128)}, u32[]{:S(2)}) copy-start(f32[2,16]{1,0:T(2,128)} %bias.1) | copy-start | bytes 388
  1.1 11.0 %copy-start.8 = (f32[2,16]{1,0:T(2,128)S(1)}, f32[2,16]{1,0:T(2,128)}, u32[]{:S(2)}) copy-start(f32[2,16]{1,0:T(2,128)} %rate.1) | copy-start | bytes 388
  1.1 11.0 %copy-start.9 = (f32[2,16]{1,0:T(2,128)S(1)}, f32[2,16]{1,0:T(2,128)}, u32[]{:S(2)}) copy-start(f32[2,16]{1,0:T(2,128)} %skip.1) | copy-start | bytes 388
  1.1 11.9 %copy-start = (bf16[2048,1024]{1,0:T(8,128)(2,1)S(1)}, bf16[2048,1024]{1,0:T(8,128)(2,1)}, u32[]{:S(2)}) copy-start(bf16[2048,1024]{1,0:T(8,128)(2,1)} %refs_2_.9) | copy-start | bytes 12582916
  1.1 11.9 %copy-start.3 = (bf16[2048,512]{1,0:T(8,128)(2,1)S(1)}, bf16[2048,512]{1,0:T(8,128)(2,1)}, u32[]{:S(2)}) copy-start(bf16[2048,512]{1,0:T(8,128)(2,1)} %refs_4_.1) | copy-start | bytes 6291460
  1.1 11.9 %copy-start.4 = (bf16[2,2048,16]{1,2,0:T(8,128)(2,1)S(1)}, bf16[2,2048,16]{1,2,0:T(8,128)(2,1)}, u32[]{:S(2)}) copy-start(bf16[2,2048,16]{1,2,0:T(8,128)(2,1)} %param.15) | copy-start | bytes 393220
  1.2 11.9 %copy-start.5 = (f32[2,4,1024]{2,1,0:T(4,128)S(1)}, f32[2,4,1024]{2,1,0:T(4,128)}, u32[]{:S(2)}) copy-start(f32[2,4,1024]{2,1,0:T(4,128)} %refs_17_.1) | copy-start | bytes 98308
  1.8 15.0 %collective-permute-start = (bf16[64,2048]{1,0:T(8,128)(2,1)S(1)}, bf16[64,2048]{1,0:T(8,128)(2,1)S(1)}, u32[]{:S(2)}, u32[]{:S(2)}) collective-permute-start(bf16[64,2048]{1,0:T(8,128)(2,1)S(1)} %get-tuple-element.70.refs_0_), channel_id=1, source_target_pairs={{0,1},{1,2},{2,3},{3,0},{4,5},{5,6},{6,7},{7,4},{8,9},{9,10},{10,1... | collective-permute-start | bytes 786440 | tf_op jit(solution)/shard_map/ppermute | solution.py:812
  4.9 14.9 %collective-permute-start.2 = (bf16[64,2048]{1,0:T(8,128)(2,1)S(1)}, bf16[64,2048]{1,0:T(8,128)(2,1)S(1)}, u32[]{:S(2)}, u32[]{:S(2)}) collective-permute-start(bf16[64,2048]{1,0:T(8,128)(2,1)S(1)} %get-tuple-element.71.refs_1_), channel_id=1, source_target_pairs={{0,3},{1,0},{2,1},{3,2},{4,7},{5,4},{6,5},{7,6},{8,11},{9,8},{10,9... | collective-permute-start | bytes 786440 | tf_op jit(solution)/shard_map/ppermute | solution.py:815
  7.0 23.8 %collective-permute-start.9 = (bf16[64,2048]{1,0:T(8,128)(2,1)S(1)}, bf16[64,2048]{1,0:T(8,128)(2,1)S(1)}, u32[]{:S(2)}, u32[]{:S(2)}) collective-permute-start(bf16[64,2048]{1,0:T(8,128)(2,1)S(1)} %get-tuple-element.71.refs_1_), channel_id=1, source_target_pairs={{0,1},{1,2},{2,3},{3,0},{4,5},{5,6},{6,7},{7,4},{8,9},{9,10},{10,1... | collective-permute-start | bytes 786440 | tf_op jit(solution)/shard_map/ppermute | solution.py:812
  7.0 5.4 %collective-permute-start.5 = (bf16[8,2048]{1,0:T(8,128)(2,1)S(1)}, bf16[8,2048]{1,0:T(8,128)(2,1)S(1)}, u32[]{:S(2)}, u32[]{:S(2)}) collective-permute-start(bf16[8,2048]{1,0:T(8,128)(2,1)S(1)} %get-tuple-element.76), channel_id=1, source_target_pairs={{3,7},{7,11},{11,15},{15,19},{19,23},{23,27},{27,31},{4,0},{8,4},{... | collective-permute-start | bytes 98312 | tf_op jit(solution)/shard_map/ppermute | solution.py:835
  8.2 32.1 %collective-permute-start.4 = (bf16[64,2048]{1,0:T(8,128)(2,1)S(1)}, bf16[64,2048]{1,0:T(8,128)(2,1)S(1)}, u32[]{:S(2)}, u32[]{:S(2)}) collective-permute-start(bf16[64,2048]{1,0:T(8,128)(2,1)S(1)} %get-tuple-element.70.refs_0_), channel_id=1, source_target_pairs={{0,3},{1,0},{2,1},{3,2},{4,7},{5,4},{6,5},{7,6},{8,11},{9,8},{10,9... | collective-permute-start | bytes 786440 | tf_op jit(solution)/shard_map/ppermute | solution.py:815
  12.3 3.8 %collective-permute-start.6 = (bf16[8,2048]{1,0:T(8,128)(2,1)S(1)}, bf16[8,2048]{1,0:T(8,128)(2,1)S(1)}, u32[]{:S(2)}, u32[]{:S(2)}) collective-permute-start(bf16[8,2048]{1,0:T(8,128)(2,1)S(1)} %get-tuple-element.76), channel_id=1, source_target_pairs={{3,4},{7,8},{11,12},{15,16},{19,20},{23,24},{27,28},{4,1},{8,5},{1... | collective-permute-start | bytes 98312 | tf_op jit(solution)/shard_map/ppermute | solution.py:835
  16.1 24.2 %collective-permute-start.7 = (bf16[8,2048]{1,0:T(8,128)(2,1)S(1)}, bf16[8,2048]{1,0:T(8,128)(2,1)S(1)}, u32[]{:S(2)}, u32[]{:S(2)}) collective-permute-start(bf16[8,2048]{1,0:T(8,128)(2,1)S(1)} %get-tuple-element.76), channel_id=1, source_target_pairs={{3,5},{7,9},{11,13},{15,17},{19,21},{23,25},{27,29},{4,2},{8,6},{1... | collective-permute-start | bytes 98312 | tf_op jit(solution)/shard_map/ppermute | solution.py:835
  16.8 23.5 %collective-permute-start.8 = (bf16[8,2048]{1,0:T(8,128)(2,1)S(1)}, bf16[8,2048]{1,0:T(8,128)(2,1)S(1)}, u32[]{:S(2)}, u32[]{:S(2)}) collective-permute-start(bf16[8,2048]{1,0:T(8,128)(2,1)S(1)} %get-tuple-element.76), channel_id=1, source_target_pairs={{3,6},{7,10},{11,14},{15,18},{19,22},{23,26},{27,30},{4,3},{8,7},{... | collective-permute-start | bytes 98312 | tf_op jit(solution)/shard_map/ppermute | solution.py:835
  19.8 25.7 %collective-permute-start.1 = (bf16[64,2048]{1,0:T(8,128)(2,1)S(1)}, bf16[64,2048]{1,0:T(8,128)(2,1)S(1)}, u32[]{:S(2)}, u32[]{:S(2)}) collective-permute-start(bf16[64,2048]{1,0:T(8,128)(2,1)S(1)} %collective-permute-done.refs_0_), channel_id=1, source_target_pairs={{0,1},{1,2},{2,3},{3,0},{4,5},{5,6},{6,7},{7,4},{8,9},{9,10},{10,1... | collective-permute-start | bytes 786440 | tf_op jit(solution)/shard_map/ppermute | solution.py:812
  30.8 14.7 %collective-permute-start.3 = (bf16[64,2048]{1,0:T(8,128)(2,1)S(1)}, bf16[64,2048]{1,0:T(8,128)(2,1)S(1)}, u32[]{:S(2)}, u32[]{:S(2)}) collective-permute-start(bf16[64,2048]{1,0:T(8,128)(2,1)S(1)} %collective-permute-done.2.refs_1_), channel_id=1, source_target_pairs={{0,3},{1,0},{2,1},{3,2},{4,7},{5,4},{6,5},{7,6},{8,11},{9,8},{10,9... | collective-permute-start | bytes 786440 | tf_op jit(solution)/shard_map/ppermute | solution.py:815
  48.7 15.0 %copy-start.1 = (bf16[2048,1024]{1,0:T(8,128)(2,1)S(1)}, bf16[2048,1024]{1,0:T(8,128)(2,1)}, u32[]{:S(2)}) copy-start(bf16[2048,1024]{1,0:T(8,128)(2,1)} %refs_2_.13) | copy-start | bytes 12582916
  50.8 4.9 %collective-permute-start.10 = (bf16[2,136,1024]{2,1,0:T(8,128)(2,1)S(1)}, bf16[2,136,1024]{2,1,0:T(8,128)(2,1)S(1)}, u32[]{:S(2)}, u32[]{:S(2)}) collective-permute-start(bf16[2,136,1024]{2,1,0:T(8,128)(2,1)S(1)} %get-tuple-element.109.mine), channel_id=1, source_target_pairs={{0,4},{4,0},{8,12},{12,8},{16,20},{20,16},{24,28},{28,24},{1,5},{5... | collective-permute-start | bytes 1671176 | tf_op jit(solution)/shard_map/ppermute | solution.py:866
  56.4 8.9 %collective-permute-start.11 = (bf16[136,512]{1,0:T(8,128)(2,1)S(1)}, bf16[136,512]{1,0:T(8,128)(2,1)S(1)}, u32[]{:S(2)}, u32[]{:S(2)}) collective-permute-start(bf16[136,512]{1,0:T(8,128)(2,1)S(1)} %get-tuple-element.110), channel_id=1, source_target_pairs={{0,8},{4,12},{8,16},{12,20},{16,24},{20,28},{24,0},{28,4},{1,9},{5... | collective-permute-start | bytes 417800 | tf_op jit(solution)/shard_map/ppermute | solution.py:876
  60.6 6.4 %collective-permute-start.12 = (bf16[136,512]{1,0:T(8,128)(2,1)S(1)}, bf16[136,512]{1,0:T(8,128)(2,1)S(1)}, u32[]{:S(2)}, u32[]{:S(2)}) collective-permute-start(bf16[136,512]{1,0:T(8,128)(2,1)S(1)} %get-tuple-element.111), channel_id=1, source_target_pairs={{0,16},{4,20},{8,24},{12,28},{16,0},{20,4},{24,8},{28,12},{1,17},{... | collective-permute-start | bytes 417800 | tf_op jit(solution)/shard_map/ppermute | solution.py:876
  60.8 8.1 %collective-permute-start.13 = (bf16[136,512]{1,0:T(8,128)(2,1)S(1)}, bf16[136,512]{1,0:T(8,128)(2,1)S(1)}, u32[]{:S(2)}, u32[]{:S(2)}) collective-permute-start(bf16[136,512]{1,0:T(8,128)(2,1)S(1)} %get-tuple-element.112), channel_id=1, source_target_pairs={{0,24},{4,28},{8,0},{12,4},{16,8},{20,12},{24,16},{28,20},{1,25},{... | collective-permute-start | bytes 417800 | tf_op jit(solution)/shard_map/ppermute | solution.py:876
  69.6 4.8 %collective-permute-start.14 = (bf16[2,128,512]{2,1,0:T(8,128)(2,1)S(1)}, bf16[2,128,512]{2,1,0:T(8,128)(2,1)S(1)}, u32[]{:S(2)}, u32[]{:S(2)}) collective-permute-start(bf16[2,128,512]{2,1,0:T(8,128)(2,1)S(1)} %entering.1.mine), channel_id=1, source_target_pairs={{0,4},{4,0},{8,12},{12,8},{16,20},{20,16},{24,28},{28,24},{1,5},{5... | collective-permute-start | bytes 786440 | tf_op jit(solution)/shard_map/ppermute | solution.py:881
  70.8 3.7 %copy-start.2 = (bf16[1024,2048]{1,0:T(8,128)(2,1)S(1)}, bf16[1024,2048]{1,0:T(8,128)(2,1)}, u32[]{:S(2)}) copy-start(bf16[1024,2048]{1,0:T(8,128)(2,1)} %w_out.7) | copy-start | bytes 12582916
  70.8 3.7 %copy-start.6 = (f32[1024]{0:T(1024)S(1)}, f32[1024]{0:T(1024)}, u32[]{:S(2)}) copy-start(f32[1024]{0:T(1024)} %param.20) | copy-start | bytes 12292
  76.3 19.0 %collective-permute-start.15 = (bf16[65,16,128]{2,1,0:T(8,128)(2,1)S(1)}, bf16[65,16,128]{2,1,0:T(8,128)(2,1)S(1)}, u32[]{:S(2)}, u32[]{:S(2)}) collective-permute-start(bf16[65,16,128]{2,1,0:T(8,128)(2,1)S(1)} %get-tuple-element.126), channel_id=1, source_target_pairs={{0,1},{1,2},{2,3},{3,0},{4,5},{5,6},{6,7},{7,4},{8,9},{9,10},{10,1... | collective-permute-start | bytes 798728 | tf_op jit(solution)/shard_map/ppermute | solution.py:812
  76.3 15.3 %collective-permute-start.19 = (bf16[65,16,128]{2,1,0:T(8,128)(2,1)S(1)}, bf16[65,16,128]{2,1,0:T(8,128)(2,1)S(1)}, u32[]{:S(2)}, u32[]{:S(2)}) collective-permute-start(bf16[65,16,128]{2,1,0:T(8,128)(2,1)S(1)} %get-tuple-element.134), channel_id=1, source_target_pairs={{0,3},{1,0},{2,1},{3,2},{4,7},{5,4},{6,5},{7,6},{8,11},{9,8},{10,9... | collective-permute-start | bytes 798728 | tf_op jit(solution)/shard_map/ppermute | solution.py:815
  83.8 15.5 %collective-permute-start.18 = (bf16[65,16,128]{2,1,0:T(8,128)(2,1)S(1)}, bf16[65,16,128]{2,1,0:T(8,128)(2,1)S(1)}, u32[]{:S(2)}, u32[]{:S(2)}) collective-permute-start(bf16[65,16,128]{2,1,0:T(8,128)(2,1)S(1)} %get-tuple-element.132), channel_id=1, source_target_pairs={{0,1},{1,2},{2,3},{3,0},{4,5},{5,6},{6,7},{7,4},{8,9},{9,10},{10,1... | collective-permute-start | bytes 798728 | tf_op jit(solution)/shard_map/ppermute | solution.py:812
  91.8 12.4 %collective-permute-start.20 = (bf16[65,16,128]{2,1,0:T(8,128)(2,1)S(1)}, bf16[65,16,128]{2,1,0:T(8,128)(2,1)S(1)}, u32[]{:S(2)}, u32[]{:S(2)}) collective-permute-start(bf16[65,16,128]{2,1,0:T(8,128)(2,1)S(1)} %plus.3), channel_id=1, source_target_pairs={{0,3},{1,0},{2,1},{3,2},{4,7},{5,4},{6,5},{7,6},{8,11},{9,8},{10,9... | collective-permute-start | bytes 798728 | tf_op jit(solution)/shard_map/ppermute | solution.py:815
  93.3 16.9 %collective-permute-start.17 = (bf16[65,16,128]{2,1,0:T(8,128)(2,1)S(1)}, bf16[65,16,128]{2,1,0:T(8,128)(2,1)S(1)}, u32[]{:S(2)}, u32[]{:S(2)}) collective-permute-start(bf16[65,16,128]{2,1,0:T(8,128)(2,1)S(1)} %get-tuple-element.131), channel_id=1, source_target_pairs={{0,3},{1,0},{2,1},{3,2},{4,7},{5,4},{6,5},{7,6},{8,11},{9,8},{10,9... | collective-permute-start | bytes 798728 | tf_op jit(solution)/shard_map/ppermute | solution.py:815
  95.4 20.2 %collective-permute-start.16 = (bf16[65,16,128]{2,1,0:T(8,128)(2,1)S(1)}, bf16[65,16,128]{2,1,0:T(8,128)(2,1)S(1)}, u32[]{:S(2)}, u32[]{:S(2)}) collective-permute-start(bf16[65,16,128]{2,1,0:T(8,128)(2,1)S(1)} %plus.2), channel_id=1, source_target_pairs={{0,1},{1,2},{2,3},{3,0},{4,5},{5,6},{6,7},{7,4},{8,9},{9,10},{10,1... | collective-permute-start | bytes 798728 | tf_op jit(solution)/shard_map/ppermute | solution.py:812
